TPU v7x, 32 devices: a whole 2x2x4 slice. The times are simulated.
32 devices in a mesh: img: 16 (over z, x, core), band: 2 (over y).
Axes of the slice: x: 2, y: 2, z: 4, core: 2. Of those that a mesh axis runs over, the one named last changes fastest.
Arguments:
- block_input: bfloat16 [16384, 1152], P(('img', 'band')), may hold values from -6 to 6
- conditioning: bfloat16 [16, 1152], P('img'), may hold values from -6 to 6
- patch_valid: int32 [16384], P(('img', 'band')), may hold values from 0 to 1, as said below
- pos_rows: int32 [16384], P(('img', 'band')), may hold values from 0 to 31, as said below
- pos_cols: int32 [16384], P(('img', 'band')), may hold values from 0 to 63, as said below
- modulation_weight: bfloat16 [1152, 6, 1152], P(None, 'band'), may hold values from -0.1875 to 0.1875
- modulation_bias: bfloat16 [6, 1152], P('band'), may hold values from -3 to 3
- attend_weight: bfloat16 [1152, 3456], replicated, may hold values from -0.1875 to 0.1875
- query_bias: bfloat16 [1152], replicated, may hold values from -3 to 3
- value_bias: bfloat16 [1152], replicated, may hold values from -3 to 3
- project_weight: bfloat16 [1152, 1152], replicated, may hold values from -1 to 1
- project_bias: bfloat16 [1152], replicated, may hold values from -3 to 3
- expand_weight: bfloat16 [1152, 4608], replicated, may hold values from -0.1875 to 0.1875
- expand_bias: bfloat16 [4608], replicated, may hold values from -3 to 3
- contract_weight: bfloat16 [4608, 1152], replicated, may hold values from -0.1875 to 0.1875
- contract_bias: bfloat16 [1152], replicated, may hold values from -3 to 3
- out_cotangent: bfloat16 [16384, 1152], P(('img', 'band')), may hold values from -6 to 6
Outputs:
- block_output: bfloat16 [16384, 1152], P(('img', 'band'))
- input_grad: float32 [16384, 1152], P(('img', 'band'))
- conditioning_grad: float32 [16, 1152], P('img')
- modulation_weight_grad: float32 [1152, 6, 1152], P('img', 'band')
- modulation_bias_grad: float32 [6, 1152], P('band')
- attend_weight_grad: float32 [1152, 3456], P('img', 'band')
- query_bias_grad: float32 [1152], replicated
- value_bias_grad: float32 [1152], replicated
- project_weight_grad: float32 [1152, 1152], P('img', 'band')
- project_bias_grad: float32 [1152], replicated
- expand_weight_grad: float32 [1152, 4608], P('img', 'band')
- expand_bias_grad: float32 [4608], replicated
- contract_weight_grad: float32 [4608, 1152], P('img', 'band')
- contract_bias_grad: float32 [1152], replicated
Inputs may be any that keep to these rules, and one draw needn't show every extreme that they name: `patch_valid`: slot s of a device belongs to the device's image s // 512. An image's grid is 16 x 2 * 32, 24 x 5 * 8 or 32 x 32 patches; band index 0 holds its upper half of rows and band index 1 its lower half, in row-major order in the first slots of the image's block, marked 1; the rest of the block is padding. `pos_rows`: the patch's row in its image's grid, 0 on padding slots. `pos_cols`: the patch's column in its image's grid, 0 on padding slots.
All inputs are finite; a program needn't handle non-finite values.
Results may differ from a plain program's by a relative error of at most 0.0147.
The roundings to bfloat16 on the way count: a program that leaves them out, or rounds other values in their place, can miss the bound.
Values may be sent and summed in bfloat16 or wider, within the bound.
A program may use at most 320 MiB of HBM per device.

v0:
```python
import functools
import math

import jax
import jax.numpy as jnp
from jax import lax
from jax.experimental import pallas as pl
from jax.sharding import PartitionSpec as P


HEADS = 16


def layer_norm(values):
    row_mean = jnp.mean(values, axis=-1, keepdims=True)
    centred = values - row_mean
    spread = jnp.mean(centred * centred, axis=-1, keepdims=True)
    return centred * lax.rsqrt(spread + 1e-06)


def gelu_tanh(values):
    return (
        0.5
        * values
        * (1.0 + jnp.tanh(0.7978845608028654 * (values + 0.044715 * values * values * values)))
    )


def swish_gate(values):
    return values / (1.0 + jnp.exp(-values))


ROW_PLACES, COL_PLACES = 32, 64


def position_pieces(features):
    quarter = features // 4
    frequency = jnp.exp(-math.log(10000.0) * jnp.arange(quarter, dtype=jnp.float32) / quarter)
    angle = jnp.arange(COL_PLACES, dtype=jnp.float32)[:, None] * frequency[None, :]
    waves = jnp.concatenate([jnp.sin(angle), jnp.cos(angle)], axis=1)
    pieces = []
    for _ in range(3):
        piece = lax.reduce_precision(waves, 8, 7)
        pieces.append(piece.astype(jnp.bfloat16))
        waves = waves - piece
    blank = jnp.zeros_like(pieces[0])
    return jnp.concatenate(
        [jnp.concatenate([piece, blank], axis=1) for piece in pieces]
        + [jnp.concatenate([blank, piece], axis=1)[:ROW_PLACES] for piece in pieces],
        axis=0,
    )


def position_table(rows_in, cols_in, pieces):
    spot = jnp.arange(pieces.shape[0])[None, :]
    col_spots = 3 * COL_PLACES
    chosen = jnp.where(
        spot < col_spots,
        spot % COL_PLACES == cols_in[:, None],
        (spot - col_spots) % ROW_PLACES == rows_in[:, None],
    )
    return jnp.dot(chosen.astype(jnp.bfloat16), pieces, preferred_element_type=jnp.float32)


def norm_modulate(values, shift_rows, scale_rows):
    return layer_norm(values) * (1.0 + scale_rows[:, None, :]) + shift_rows[:, None, :]


def swap_bit(value, bit):
    members = lax.axis_size("img")
    return lax.ppermute(value, "img", [(i, i ^ (1 << bit)) for i in range(members)])


def swap_band(value):
    return lax.ppermute(value, "band", [(0, 1), (1, 0)])


def swap(value, stage):
    return swap_band(value) if stage == "band" else swap_bit(value, stage)


def my_bit(stage):
    if stage == "band":
        return lax.axis_index("band")
    return (lax.axis_index("img") >> stage) & 1


def pick(choice, if_zero, if_one):
    return jnp.where(choice == 0, if_zero, if_one)


def image_bits():
    return lax.axis_size("img").bit_length() - 1


def attend_kernel(score_scale, q_ref, k_ref, v_ref, kx_ref, vx_ref, mask_ref, out_ref, log_ref):
    keys = jnp.concatenate([k_ref[0], kx_ref[0]], axis=1)
    values = jnp.concatenate([v_ref[0], vx_ref[0]], axis=1)
    scores = lax.dot_general(
        keys, q_ref[0], (((0,), (0,)), ((), ())), preferred_element_type=jnp.float32
    )
    scores = jnp.where(mask_ref[...] > 0, scores * score_scale, -1e30)
    top = jnp.max(scores, axis=0, keepdims=True)
    weights = jnp.exp(scores - top)
    total = jnp.sum(weights, axis=0, keepdims=True)
    probabilities = (weights * (1.0 / total)).astype(jnp.bfloat16)
    out_ref[0] = jnp.dot(values, probabilities, preferred_element_type=jnp.float32).astype(
        jnp.bfloat16
    )
    log_ref[0] = top + jnp.log(total)


def head_blocks(size, rows, heads):
    block = lambda base: pl.BlockSpec((1, size, rows), lambda h: (base * heads + h, 0, 0))
    return [block(0), block(1), block(2), block(0), block(1)]


def attend_forward(own, other, mask, score_scale):
    heads, (_, size, rows) = HEADS, own.shape
    columns = 2 * rows
    return pl.pallas_call(
        functools.partial(attend_kernel, score_scale),
        grid=(heads,),
        in_specs=head_blocks(size, rows, heads)
        + [pl.BlockSpec((columns, 1), lambda h: (0, 0))],
        out_specs=[
            pl.BlockSpec((1, size, rows), lambda h: (h, 0, 0)),
            pl.BlockSpec((1, 1, rows), lambda h: (h, 0, 0)),
        ],
        out_shape=[
            jax.ShapeDtypeStruct((heads, size, rows), jnp.bfloat16),
            jax.ShapeDtypeStruct((heads, 1, rows), jnp.float32),
        ],
        cost_estimate=pl.CostEstimate(
            flops=16 * heads * 128 * rows * columns,
            bytes_accessed=4 * heads * size * (rows + columns),
            transcendentals=heads * rows * columns,
        ),
    )(own, own, own, other, other, mask)


def attend_back_kernel(
    score_scale,
    q_ref,
    k_ref,
    v_ref,
    kx_ref,
    vx_ref,
    go_ref,
    log_ref,
    mask_ref,
    dq_ref,
    own_ref,
    other_ref,
):
    queries, grads = q_ref[0], go_ref[0]
    keys = jnp.concatenate([k_ref[0], kx_ref[0]], axis=1)
    values = jnp.concatenate([v_ref[0], vx_ref[0]], axis=1)
    rows = queries.shape[1]

    def outer(left, right):
        return lax.dot_general(
            left, right, (((0,), (0,)), ((), ())), preferred_element_type=jnp.float32
        )

    def across(left, right):
        return lax.dot_general(
            left, right, (((1,), (1,)), ((), ())), preferred_element_type=jnp.float32
        )

    scores = jnp.where(mask_ref[...] > 0, outer(keys, queries) * score_scale, -1e30)
    weights = jnp.exp(scores - log_ref[0])
    grad_weights = outer(values, grads)
    delta = jnp.sum(weights * grad_weights, axis=0, keepdims=True)
    grad_scores = (weights * (grad_weights - delta)).astype(jnp.bfloat16)
    grad_values = across(grads, weights.astype(jnp.bfloat16))
    grad_keys = across(queries, grad_scores) * score_scale
    for i, grad in enumerate((grad_keys, grad_values)):
        own_ref[i, 0] = grad[:, :rows]
        other_ref[i, 0] = grad[:, rows:].astype(other_ref.dtype)
    dq_ref[0] = (
        jnp.dot(keys, grad_scores, preferred_element_type=jnp.float32) * score_scale
    ).astype(dq_ref.dtype)


def attend_backward(own, other, grads, log_total, mask, score_scale):
    heads, (_, size, rows) = HEADS, own.shape
    columns = 2 * rows
    single = pl.BlockSpec((1, size, rows), lambda h: (h, 0, 0))
    double = pl.BlockSpec((2, 1, size, rows), lambda h: (0, h, 0, 0))
    return pl.pallas_call(
        functools.partial(attend_back_kernel, score_scale),
        grid=(heads,),
        in_specs=head_blocks(size, rows, heads)
        + [
            single,
            pl.BlockSpec((1, 1, rows), lambda h: (h, 0, 0)),
            pl.BlockSpec((columns, 1), lambda h: (0, 0)),
        ],
        out_specs=[single, double, double],
        out_shape=[
            jax.ShapeDtypeStruct((heads, size, rows), jnp.bfloat16),
            jax.ShapeDtypeStruct((2, heads, size, rows), jnp.float32),
            jax.ShapeDtypeStruct((2, heads, size, rows), jnp.bfloat16),
        ],
        cost_estimate=pl.CostEstimate(
            flops=30 * heads * 128 * rows * columns,
            bytes_accessed=8 * heads * size * (rows + columns),
            transcendentals=heads * rows * columns,
        ),
    )(own, own, own, other, other, grads, log_total, mask)


def column_tile(width):
    return 384 if width % 384 == 0 else width


def project_kernel(rows_ref, weight_ref, bias_ref, out_ref):
    flat = jnp.dot(rows_ref[...], weight_ref[...], preferred_element_type=jnp.float32)
    out_ref[...] = (flat + bias_ref[...].astype(jnp.float32)).T.astype(out_ref.dtype)


def project_rows(rows, weight, bias, skip):
    depth = weight.shape[0]
    width = weight.shape[1] - skip
    tile = column_tile(depth)
    first = skip // tile
    return pl.pallas_call(
        project_kernel,
        grid=(width // tile,),
        in_specs=[
            pl.BlockSpec(rows.shape, lambda n: (0, 0)),
            pl.BlockSpec((depth, tile), lambda n: (0, n + first)),
            pl.BlockSpec((1, tile), lambda n: (0, n + first)),
        ],
        out_specs=pl.BlockSpec((tile, rows.shape[0]), lambda n: (n, 0)),
        out_shape=jax.ShapeDtypeStruct((width, rows.shape[0]), jnp.bfloat16),
        cost_estimate=pl.CostEstimate(
            flops=2 * rows.shape[0] * depth * width,
            bytes_accessed=2 * depth * width,
            transcendentals=0,
        ),
    )(rows, weight, bias)


def product_kernel(
    left_axis, right_axis, columns, orders, per_step, left_ref, left_far, right_ref,
    right_far, *out_refs
):
    contract = (((left_axis,), (right_axis,)), ((), ()))
    near = lax.dot_general(
        left_ref[...], right_ref[...], contract, preferred_element_type=jnp.float32
    )
    far = lax.dot_general(
        left_far[...], right_far[...], contract, preferred_element_type=jnp.float32
    )
    total = (near + far).astype(jnp.bfloat16)
    padded = total.shape[1] // 2
    chunk = total.shape[0] // per_step
    part = chunk // len(orders)

    def piece(band, index, i):
        start = index * chunk + i * part
        return total[start : start + part, band * padded : band * padded + columns]

    for i, order in enumerate(orders):
        going_ref, staying_ref = out_refs[2 * i], out_refs[2 * i + 1]
        if order[0] == "band":
            for index in range(per_step):
                going_ref[index] = piece(0, index, i)
                staying_ref[index] = piece(1, index, i)
        else:
            side = (lax.axis_index("img") >> order[0]) & 1
            step = 1 << (order[0] - 1)
            slot = 0
            for index in range(per_step):
                if index & step:
                    continue
                for band in range(2):
                    first, second = piece(band, index, i), piece(band, index | step, i)
                    going_ref[band, slot] = jnp.where(side == 0, second, first)
                    staying_ref[band, slot] = jnp.where(side == 0, first, second)
                slot += 1


def row_product(left, left_far, right, right_far, left_axis, right_axis, columns, orders):
    depth, width = left.shape[left_axis], left.shape[1 - left_axis]
    bits = image_bits()
    chunks = 1 << (bits - 1)
    tile = width // 4 if width > 2 * right.shape[1 - right_axis] else width
    per_step = chunks * tile // width
    part = width // chunks // len(orders)
    left_block = (
        pl.BlockSpec((depth, tile), lambda k: (0, k))
        if left_axis == 0
        else pl.BlockSpec((tile, depth), lambda k: (k, 0))
    )
    right_block = pl.BlockSpec(right.shape, lambda k: (0, 0))
    out_specs, out_shape = [], []
    for order in orders:
        if order[0] == "band":
            shape, block = (chunks, part, columns), (per_step, part, columns)
            spec = pl.BlockSpec(block, lambda k: (k, 0, 0))
        else:
            shape = (2, chunks // 2, part, columns)
            spec = pl.BlockSpec((2, per_step // 2, part, columns), lambda k: (0, k, 0, 0))
        out_specs += [spec, spec]
        out_shape += [jax.ShapeDtypeStruct(shape, jnp.bfloat16)] * 2
    outs = pl.pallas_call(
        functools.partial(
            product_kernel, left_axis, right_axis, columns, orders, per_step
        ),
        grid=(width // tile,),
        in_specs=[left_block, left_block, right_block, right_block],
        out_specs=out_specs,
        out_shape=out_shape,
        cost_estimate=pl.CostEstimate(
            flops=8 * depth * width * columns,
            bytes_accessed=8 * depth * (width + columns) + 4 * width * columns,
            transcendentals=0,
        ),
    )(left, left_far, right, right_far)
    halves = []
    for i, order in enumerate(orders):
        left_bits = ["band"] + list(range(bits - 1, 0, -1))
        left_bits.remove(order[0])
        shape = (2,) * len(left_bits) + (part, columns)
        halves.append((outs[2 * i].reshape(shape), outs[2 * i + 1].reshape(shape)))
    return halves


def core_columns(values, axis, core, band):
    quarter = values.shape[axis] // 4
    pieces = [lax.slice_in_dim(values, i * quarter, (i + 1) * quarter, axis=axis) for i in range(4)]
    return pick(
        band, pick(core, pieces[0], pieces[1]), pick(core, pieces[2], pieces[3])
    )


def halved_kernel(columns, part, left_ref, left_far, right_ref, right_far, going_ref, staying_ref):
    core = lax.axis_index("img") & 1
    chips = left_ref.shape[1] // (2 * part)

    def own_rows(ref):
        rows = ref[...].T
        pieces = [rows[i * part : (i + 1) * part] for i in range(2 * chips)]
        return jnp.concatenate(
            [jnp.where(core == 0, pieces[2 * i], pieces[2 * i + 1]) for i in range(chips)], axis=0
        )

    near = jnp.dot(own_rows(left_ref), right_ref[...], preferred_element_type=jnp.float32)
    far = jnp.dot(own_rows(left_far), right_far[...], preferred_element_type=jnp.float32)
    total = (near + far).astype(jnp.bfloat16)
    padded = total.shape[1] // 2
    side = (lax.axis_index("img") >> 1) & 1
    for i in range(2):
        pieces = [
            total[x * part : (x + 1) * part, i * padded : i * padded + columns]
            for x in range(chips)
        ]
        for x in range(chips // 2):
            first, second = pieces[2 * x], pieces[2 * x + 1]
            going_ref[i, x] = jnp.where(side == 0, second, first)
            staying_ref[i, x] = jnp.where(side == 0, first, second)


def halved_product(left, right):
    depth, width = left.shape
    bits = image_bits()
    chips = 1 << (bits - 1)
    band = my_bit("band")
    columns = right.shape[1] // 2
    halves = [right[:, :columns], right[:, columns:]]
    right = jnp.concatenate(
        [
            jnp.pad(pick(band, *pair), [(0, 0), (0, -columns % 128)])
            for pair in (halves[::-1], halves)
        ],
        axis=1,
    )
    right_far = swap_bit(right, 0)
    tile, part = width // 4, width // chips // 2
    left_block = pl.BlockSpec((depth, tile), lambda k: (0, k))
    right_block = pl.BlockSpec(right.shape, lambda k: (0, 0))
    out_block = pl.BlockSpec((2, chips // 8, part, columns), lambda k: (0, k, 0, 0))
    out_shape = jax.ShapeDtypeStruct((2, chips // 2, part, columns), jnp.bfloat16)
    going, staying = pl.pallas_call(
        functools.partial(halved_kernel, columns, part),
        grid=(4,),
        in_specs=[left_block, left_block, right_block, right_block],
        out_specs=[out_block, out_block],
        out_shape=[out_shape, out_shape],
        cost_estimate=pl.CostEstimate(
            flops=4 * depth * width * columns,
            bytes_accessed=8 * depth * (width + columns) + 4 * width * columns,
            transcendentals=0,
        ),
    )(left, swap_bit(left, 0), right, right_far)
    shape = (2,) * (bits - 1) + (part, columns)
    return going.reshape(shape), staying.reshape(shape)


def chip_product(left, right, orders, left_axis=0, right_axis=0):
    core, band = my_bit(0), my_bit("band")
    axis = 1 - right_axis
    columns = right.shape[axis] // 4
    edges = [(0, 0), (0, 0)]
    edges[axis] = (0, -columns % 128)

    def chosen(which):
        return jnp.concatenate(
            [jnp.pad(core_columns(right, axis, which, b), edges) for b in (1 - band, band)],
            axis=axis,
        )

    left_far, right_far = swap_bit(left, 0), swap_bit(chosen(1 - core), 0)
    return row_product(
        left, left_far, chosen(core), right_far, left_axis, right_axis, columns, orders
    )


def scatter_sum(halves, orders):
    core = my_bit(0)
    totals = [scatter_part(*pair, order) for pair, order in zip(halves, orders)]
    total = jnp.concatenate(totals, axis=0) if len(totals) > 1 else totals[0]
    rows = total.shape[0] // 2
    low, high = total[:rows], total[rows:]
    here, there = pick(core, low, high), swap_bit(pick(core, high, low), 0)
    return pick(
        core,
        jnp.concatenate([here, there], axis=1),
        jnp.concatenate([there, here], axis=1),
    )


def scatter_part(going, staying, order):
    alive = ["band"] + list(range(image_bits() - 1, 0, -1))
    for stage in order:
        axis = alive.index(stage)
        alive.remove(stage)
        if stage != order[0]:
            first = lax.index_in_dim(block, 0, axis, keepdims=False)
            second = lax.index_in_dim(block, 1, axis, keepdims=False)
            if stage == "band":
                going, staying = first, second
            else:
                side = my_bit(stage)
                going, staying = pick(side, second, first), pick(side, first, second)
        arrived = swap(going, stage)
        block = staying.astype(jnp.float32) + arrived.astype(jnp.float32)
        if stage != order[-1]:
            block = block.astype(jnp.bfloat16)
    return block


def sum_all(value):
    for stage in ["band"] + list(range(image_bits())):
        value = value + swap(value, stage)
    return value


def gather_images(value):
    for stage in range(image_bits()):
        other = swap_bit(value, stage)
        side = my_bit(stage)
        value = jnp.concatenate([pick(side, value, other), pick(side, other, value)], axis=0)
    return value


def shards(
    block_input,
    conditioning,
    patch_valid,
    pos_rows,
    pos_cols,
    modulation_weight,
    modulation_bias,
    attend_weight,
    query_bias,
    value_bias,
    project_weight,
    project_bias,
    expand_weight,
    expand_bias,
    contract_weight,
    contract_bias,
    out_cotangent,
):
    slot_count, features = block_input.shape
    image_count = conditioning.shape[0]
    per_image = slot_count // image_count
    head_count = HEADS
    rest = list(range(3, image_bits()))
    expand_order = [2, 1, "band"] + rest
    contract_order = [1, 2, "band"] + rest
    project_order = ["band", 2, 1] + rest
    attend_orders = [[1, "band", 2] + rest, ["band", 2, 1] + rest, [2, 1, "band"] + rest]
    head_size = features // head_count
    score_scale = 1.0 / math.sqrt(head_size)
    valid_rows = patch_valid.astype(jnp.float32)
    band = lax.axis_index("band")
    other_places = swap_band(jnp.stack([pos_rows, pos_cols, patch_valid]))
    sent_input, other_places = lax.optimization_barrier((block_input, other_places))
    other_input = swap_band(sent_input)
    pieces = position_pieces(features)
    pos_table = position_table(pos_rows, pos_cols, pieces)
    other_table = position_table(other_places[0], other_places[1], pieces)
    hidden = block_input.astype(jnp.float32) + pos_table
    shaped = hidden.reshape(image_count, per_image, features)
    cond_float = conditioning.astype(jnp.float32)
    swish_value, swish_back = jax.vjp(swish_gate, cond_float)
    activated = swish_value.astype(jnp.bfloat16)
    modulation_half = jnp.einsum(
        "id,dkc->ikc", activated, modulation_weight, preferred_element_type=jnp.float32
    ) + modulation_bias.astype(jnp.float32)
    modulation_other = swap_band(modulation_half)
    modulation = jnp.concatenate(
        [
            pick(band, modulation_half, modulation_other),
            pick(band, modulation_other, modulation_half),
        ],
        axis=1,
    )
    shift_one, scale_one, gate_one = (modulation[:, 0], modulation[:, 1], modulation[:, 2])
    shift_two, scale_two, gate_two = (modulation[:, 3], modulation[:, 4], modulation[:, 5])
    first_mod, first_back = jax.vjp(norm_modulate, shaped, shift_one, scale_one)
    first_low = first_mod.astype(jnp.bfloat16).reshape(slot_count, features)
    input_bias = jnp.concatenate([query_bias, jnp.zeros_like(query_bias), value_bias])[None, :]

    def project_heads(rows, skip):
        flat = project_rows(rows, attend_weight, input_bias, skip)
        return flat.reshape(-1, head_size, slot_count)

    own_heads = project_heads(first_low, 0)
    other_shaped = (other_input.astype(jnp.float32) + other_table).reshape(
        image_count, per_image, features
    )
    other_low = (
        norm_modulate(other_shaped, shift_one, scale_one)
        .astype(jnp.bfloat16)
        .reshape(slot_count, features)
    )
    other_heads = project_heads(other_low, features)
    key_mask = jnp.concatenate([patch_valid, other_places[2]]).astype(jnp.float32)[:, None]
    mixed_heads, log_total = attend_forward(own_heads, other_heads, key_mask, score_scale)
    mixed_low = mixed_heads.reshape(features, slot_count)
    branch = jnp.einsum(
        "et,ed->td", mixed_low, project_weight, preferred_element_type=jnp.float32
    ) + project_bias.astype(jnp.float32)
    branch_rows = branch.reshape(image_count, per_image, features)
    middle = shaped + gate_one[:, None, :] * branch_rows
    second_mod, second_back = jax.vjp(norm_modulate, middle, shift_two, scale_two)
    second_low = second_mod.astype(jnp.bfloat16).reshape(slot_count, features)
    expanded = jnp.dot(
        second_low, expand_weight, preferred_element_type=jnp.float32
    ) + expand_bias.astype(jnp.float32)
    activation, gelu_back = jax.vjp(gelu_tanh, expanded)
    activation_low = activation.astype(jnp.bfloat16)
    mlp_out = jnp.dot(
        activation_low, contract_weight, preferred_element_type=jnp.float32
    ) + contract_bias.astype(jnp.float32)
    mlp_rows = mlp_out.reshape(image_count, per_image, features)
    result = middle + gate_two[:, None, :] * mlp_rows
    block_output = result.reshape(slot_count, features).astype(jnp.bfloat16)
    upstream = (out_cotangent.astype(jnp.float32) * valid_rows[:, None]).reshape(
        image_count, per_image, features
    )
    grad_gate_two = jnp.sum(upstream * mlp_rows, axis=1)
    grad_mlp = (gate_two[:, None, :] * upstream).reshape(slot_count, features).astype(jnp.bfloat16)
    contract_chip = halved_product(activation_low, grad_mlp)
    contract_bias_grad = jnp.sum(grad_mlp.astype(jnp.float32), axis=0)
    grad_activation = jnp.einsum(
        "td,fd->tf", grad_mlp, contract_weight, preferred_element_type=jnp.float32
    )
    grad_expanded = gelu_back(grad_activation)[0].astype(jnp.bfloat16)
    expand_chip = chip_product(second_low, grad_expanded, [expand_order])
    expand_bias_grad = jnp.sum(grad_expanded.astype(jnp.float32), axis=0)
    grad_second = jnp.einsum(
        "tf,df->td", grad_expanded, expand_weight, preferred_element_type=jnp.float32
    )
    grad_norm_two, grad_shift_two, grad_scale_two = second_back(
        grad_second.reshape(image_count, per_image, features)
    )
    grad_middle = upstream + grad_norm_two
    grad_gate_one = jnp.sum(grad_middle * branch_rows, axis=1)
    grad_branch = (
        (gate_one[:, None, :] * grad_middle).reshape(slot_count, features).astype(jnp.bfloat16)
    )
    grad_branch, contract_chip, expand_chip = lax.optimization_barrier(
        (grad_branch, contract_chip, expand_chip)
    )
    contract_out = scatter_part(*contract_chip, contract_order)
    expand_out = scatter_sum(expand_chip, [expand_order])
    project_chip = chip_product(mixed_low, grad_branch, [project_order], left_axis=1)
    project_out = scatter_sum(project_chip, [project_order])
    project_bias_grad = jnp.sum(grad_branch.astype(jnp.float32), axis=0)
    grad_mixed = jnp.einsum(
        "td,ed->et", grad_branch, project_weight, preferred_element_type=jnp.float32
    ).astype(jnp.bfloat16)
    grad_query, grad_pair, grad_pair_other = attend_backward(
        own_heads,
        other_heads,
        grad_mixed.reshape(head_count, head_size, slot_count),
        log_total,
        key_mask,
        score_scale,
    )
    grad_pair_far = swap_band(grad_pair_other)
    grad_pair = grad_pair + grad_pair_far.astype(jnp.float32)
    grad_qkv = jnp.concatenate(
        [
            grad_query.reshape(features, slot_count),
            grad_pair.astype(jnp.bfloat16).reshape(2 * features, slot_count),
        ],
        axis=0,
    )
    attend_chip = chip_product(first_low, grad_qkv, attend_orders, right_axis=1)
    attend_out = scatter_sum(attend_chip, attend_orders)
    query_bias_grad = jnp.sum(grad_qkv[:features].astype(jnp.float32), axis=1)
    value_bias_grad = jnp.sum(grad_qkv[2 * features :].astype(jnp.float32), axis=1)
    grad_first = jnp.einsum(
        "et,de->td", grad_qkv, attend_weight, preferred_element_type=jnp.float32
    )
    grad_norm_one, grad_shift_one, grad_scale_one = first_back(
        grad_first.reshape(image_count, per_image, features)
    )
    input_grad = (grad_middle + grad_norm_one).reshape(slot_count, features)
    grad_modulation = jnp.stack(
        [
            grad_shift_one,
            grad_scale_one,
            grad_gate_one,
            grad_shift_two,
            grad_scale_two,
            grad_gate_two,
        ],
        axis=1,
    )
    grad_halves = grad_modulation.reshape(image_count, 2, -1, features)
    modulation_grad_half = (
        pick(band, grad_halves[:, 0], grad_halves[:, 1])
        + swap_band(pick(band, grad_halves[:, 1], grad_halves[:, 0]))
    ).astype(jnp.bfloat16)
    activated_grad_part = jnp.einsum(
        "ikc,dkc->id", modulation_grad_half, modulation_weight, preferred_element_type=jnp.float32
    )
    conditioning_grad = swish_back(activated_grad_part + swap_band(activated_grad_part))[0]
    all_grads = gather_images(modulation_grad_half)
    all_activated = gather_images(activated)
    block_rows = features // lax.axis_size("img")
    own_activated = lax.dynamic_slice_in_dim(
        all_activated, lax.axis_index("img") * block_rows, block_rows, axis=1
    )
    modulation_grad_out = jnp.einsum(
        "id,ikc->dkc", own_activated, all_grads, preferred_element_type=jnp.float32
    )
    modulation_bias_out = jnp.sum(all_grads.astype(jnp.float32), axis=0)
    bias_parts = [
        query_bias_grad,
        value_bias_grad,
        project_bias_grad,
        expand_bias_grad,
        contract_bias_grad,
    ]
    bias_total = sum_all(jnp.concatenate(bias_parts))
    bias_outs = []
    place = 0
    for part in bias_parts:
        bias_outs.append(bias_total[place : place + part.shape[0]])
        place += part.shape[0]
    (
        query_bias_out,
        value_bias_out,
        project_bias_out,
        expand_bias_out,
        contract_bias_out,
    ) = bias_outs
    return (
        block_output,
        input_grad,
        conditioning_grad,
        modulation_grad_out,
        modulation_bias_out,
        attend_out,
        query_bias_out,
        value_bias_out,
        project_out,
        project_bias_out,
        expand_out,
        expand_bias_out,
        contract_out,
        contract_bias_out,
    )


def solution(mesh):
    in_specs = (
        P(("img", "band"), None),
        P("img", None),
        P(("img", "band")),
        P(("img", "band")),
        P(("img", "band")),
        P(None, "band", None),
        P("band", None),
        P(),
        P(),
        P(),
        P(),
        P(),
        P(),
        P(),
        P(),
        P(),
        P(("img", "band"), None),
    )
    out_specs = (
        P(("img", "band"), None),
        P(("img", "band"), None),
        P("img", None),
        P("img", "band", None),
        P("band", None),
        P("img", "band"),
        P(),
        P(),
        P("img", "band"),
        P(),
        P("img", "band"),
        P(),
        P("img", "band"),
        P(),
    )

    return jax.shard_map(shards, mesh=mesh, in_specs=in_specs, out_specs=out_specs, check_vma=False)
```

profile of v0, /device:TPU:0, one launch (start us, length us, event | category | flops | bytes accessed | tf_op | source)
XLA Modules:
  0.0 458.0 jit_solution(17549033092148527558)
XLA Ops:
  4.7 4.4 fusion.79
  31.5 14.0 %collective-permute-done.2 = bf16[512,1152]{1,0:T(8,128)(2,1)} collective-permute-done((bf16[512,1152]{1,0:T(8,128)(2,1)}, bf16[512,1152]{1,0:T(8,128)(2,1)}, u32[]{:S(2)}, u32[]{:S(2)}) %collective-permute-start.2) | collective-permute-done | bytes 1179680 | tf_op jit(solution)/shard_map/ppermute | solution.py:75
  53.4 12.5 %shard_map.272 = bf16[3456,512]{1,0:T(8,128)(2,1)} custom-call(bf16[512,1152]{1,0:T(8,128)(2,1)} %get-tuple-element.130.rows_ref.left_ref, bf16[1152,3456]{1,0:T(8,128)(2,1)} %weight_ref.3, bf16[1,3456]{1,0:T(2,128)(2,1)} %broadcast_in_dim.27.bias_ref), custom_call_target="tpu_custom_call" | custom-call | flops 4076863488 | bytes 7962624 | tf_op jit(solution)/shard_map/pallas_call | solution.py:228
  65.9 8.8 %shard_map.273 = bf16[2304,512]{1,0:T(8,128)(2,1)} custom-call(bf16[512,1152]{1,0:T(8,128)(2,1)} %get-tuple-element.129.rows_ref, bf16[1152,3456]{1,0:T(8,128)(2,1)} %weight_ref.3, bf16[1,3456]{1,0:T(2,128)(2,1)} %broadcast_in_dim.27.bias_ref), custom_call_target="tpu_custom_call" | custom-call | flops 2717908992 | bytes 5308416 | tf_op jit(solution)/shard_map/pallas_call | solution.py:228
  74.8 21.4 %shard_map.274 = (bf16[16,72,512]{2,1,0:T(8,128)(2,1)}, f32[16,1,512]{2,1,0:T(1,128)}) custom-call(bf16[48,72,512]{2,1,0:T(8,128)(2,1)} %bitcast.216, bf16[48,72,512]{2,1,0:T(8,128)(2,1)} %bitcast.217, bf16[48,72,512]{2,1,0:T(8,128)(2,1)} %bitcast.218, bf16[32,72,512]{2,1,0:T(8,128)(2,1)} %bitcast.195, bf16[32,72,512]{2,1,0:T(8,128)(2,1)} %bitcast.196, ...), custom_call_target="tpu_custom_call" | custom-call | flops 17179869184 | bytes 7077888 | tf_op jit(solution)/shard_map/pallas_call | solution.py:121
  96.2 5.5 %fusion.97 = (f32[512]{0:T(512)S(1)}, f32[512,1152]{1,0:T(8,128)S(1)}, f32[512,1152]{1,0:T(8,128)}) fusion(f32[512,1152]{1,0:T(8,128)} %copy-done.2, f32[1152]{0:T(1024)S(1)} %get-tuple-element.73, f32[1152]{0:T(1024)S(1)} %convert_element_type.401, bf16[1152,512]{1,0:T(8,128)(2,1)} %bitcast.11.left_ref, bf16[1152,1152]{1,0:T(8,128)(2,1)S(1)} %copy-done), kind=kOutput, calls=%fused_computation.308 | convolution fusion | flops 1361313280 | bytes 10923008 | tf_op jit(solution)/shard_map/et,ed->td/dot_general | solution.py:547
  103.6 11.4 %fusion.100 = f32[512,4608]{1,0:T(8,128)} fusion(bf16[512,1152]{1,0:T(8,128)(2,1)} %add_convert_fusion.4.left_ref, bf16[1152,4608]{1,0:T(8,128)(2,1)} %param.29), kind=kOutput, calls=%fused_computation.311 | convolution fusion | flops 5435817984 | bytes 21233664 | tf_op jit(solution)/shard_map/dot_general | solution.py:554
  115.0 20.6 %convert_reduce_fusion = (f32[4608]{0:T(1024)}, bf16[512,4608]{1,0:T(8,128)(2,1)S(1)}, bf16[512,4608]{1,0:T(8,128)(2,1)}) fusion(f32[512,4608]{1,0:T(8,128)} %fusion.100, f32[4608]{0:T(1024)S(1)} %convert_element_type.403, bf16[512,1152]{1,0:T(8,128)(2,1)} %copy-done.19, bf16[4608,1152]{1,0:T(8,128)(2,1)} %param.31), kind=kOutput, calls=%fused_computation.10 | convolution fusion | flops 5504232960 | bytes 30707712 | tf_op jit(solution)/shard_map/td,fd->tf/dot_general | solution.py:572
  138.2 11.2 %multiply_reduce_fusion.1 = (f32[1152]{0:T(1024)}, f32[512]{0:T(512)S(1)}, f32[1152]{0:T(1024)}, f32[512,1152]{1,0:T(8,128)S(1)}) fusion(f32[512,1152]{1,0:T(8,128)S(1)} %get-tuple-element.87, f32[512]{0:T(512)S(1)} %fusion.90, f32[512]{0:T(512)S(1)} %broadcast_multiply_fusion, f32[1152]{0:T(1024)S(1)} %get-tuple-element.72, ...), kind=kOutput, calls=%fused_computation.47 | convolution fusion | flops 5440534016 | bytes 20073984 | tf_op jit(solution)/shard_map/tf,df->td/dot_general | solution.py:578
  154.7 11.2 %shard_map.276 = (bf16[2,4,144,1152]{3,2,1,0:T(8,128)(2,1)}, bf16[2,4,144,1152]{3,2,1,0:T(8,128)(2,1)}) custom-call(bf16[512,1152]{1,0:T(8,128)(2,1)} %add_convert_fusion.4.left_ref, bf16[512,1152]{1,0:T(8,128)(2,1)} %collective-permute-done.5.left_far, bf16[512,2304]{1,0:T(8,128)(2,1)} %pad_maximum_fusion.right_ref, ...), custom_call_target="tpu_custom_call" | custom-call | flops 5435817984 | bytes 14745600 | tf_op jit(solution)/shard_map/pallas_call | solution.py:309
  165.9 11.4 %shard_map.275 = (bf16[2,4,288,576]{3,2,1,0:T(8,128)(2,1)}, bf16[2,4,288,576]{3,2,1,0:T(8,128)(2,1)}) custom-call(bf16[512,4608]{1,0:T(8,128)(2,1)} %get-tuple-element.88.left_ref, bf16[512,4608]{1,0:T(8,128)(2,1)} %collective-permute-done.3.left_far, bf16[512,1280]{1,0:T(8,128)(2,1)} %fusion.31.right_ref, bf16[512,1280]{1,0:T(8,128)(2,1)} %collective-permute-done.4.right_far), custom_call_target="tpu_custom_call" | custom-call | flops 5435817984 | bytes 31850496 | tf_op jit(solution)/shard_map/pallas_call | solution.py:387
  187.2 5.3 %shard_map.279 = (bf16[8,144,288]{2,1,0:T(8,128)(2,1)}, bf16[8,144,288]{2,1,0:T(8,128)(2,1)}) custom-call(bf16[1152,512]{1,0:T(8,128)(2,1)} %bitcast.11.left_ref, bf16[1152,512]{1,0:T(8,128)(2,1)} %collective-permute-done.38.left_far, bf16[512,768]{1,0:T(8,128)(2,1)} %fusion.34.right_ref, bf16[512,768]{1,0:T(8,128)(2,1)} %collective-permute-done.39.right_far), custom_call_target="tpu_custom_call" | custom-call | flops 1358954496 | bytes 7225344 | tf_op jit(solution)/shard_map/pallas_call | solution.py:309
  195.4 31.6 %shard_map.277 = (bf16[16,72,512]{2,1,0:T(8,128)(2,1)}, f32[2,16,72,512]{3,2,1,0:T(8,128)}, bf16[2,16,72,512]{3,2,1,0:T(8,128)(2,1)}) custom-call(bf16[48,72,512]{2,1,0:T(8,128)(2,1)} %bitcast.219, bf16[48,72,512]{2,1,0:T(8,128)(2,1)} %bitcast.220, bf16[48,72,512]{2,1,0:T(8,128)(2,1)} %bitcast.221, bf16[32,72,512]{2,1,0:T(8,128)(2,1)} %bitcast.197, ...), custom_call_target="tpu_custom_call" | custom-call | flops 32212254720 | bytes 14155776 | tf_op jit(solution)/shard_map/pallas_call | solution.py:191
  232.1 9.0 %collective-permute-done.41 = bf16[2,2,144,288]{3,2,0,1:T(8,128)(2,1)S(1)} collective-permute-done((bf16[2,2,144,288]{3,2,0,1:T(8,128)(2,1)S(1)}, bf16[2,2,144,288]{3,2,0,1:T(8,128)(2,1)S(1)}, u32[]{:S(2)}, u32[]{:S(2)}) %collective-permute-start.41) | collective-permute-done | bytes 331808 | tf_op jit(solution)/shard_map/ppermute | solution.py:71
  242.6 5.3 %collective-permute-done.42 = bf16[2,144,288]{2,1,0:T(8,128)(2,1)S(1)} collective-permute-done((bf16[2,144,288]{2,1,0:T(8,128)(2,1)S(1)}, bf16[2,144,288]{2,1,0:T(8,128)(2,1)S(1)}, u32[]{:S(2)}, u32[]{:S(2)}) %collective-permute-start.42) | collective-permute-done | bytes 165920 | tf_op jit(solution)/shard_map/ppermute | solution.py:71
  261.3 19.6 %collective-permute-done.7 = bf16[2,16,72,512]{3,2,1,0:T(8,128)(2,1)} collective-permute-done((bf16[2,16,72,512]{3,2,1,0:T(8,128)(2,1)}, bf16[2,16,72,512]{3,2,1,0:T(8,128)(2,1)}, u32[]{:S(2)}, u32[]{:S(2)}) %collective-permute-start.7) | collective-permute-done | bytes 2359328 | tf_op jit(solution)/shard_map/ppermute | solution.py:75
  280.9 4.0 add_convert_fusion.2
  287.4 11.3 %multiply_reduce_fusion.3 = (f32[1152]{0:T(1024)S(1)}, f32[512]{0:T(512)S(1)}, f32[1152]{0:T(1024)S(1)}, f32[512,1152]{1,0:T(8,128)}) fusion(f32[512,1152]{1,0:T(8,128)S(1)} %copy-done.4, f32[512]{0:T(512)S(1)} %copy-done.49, f32[512]{0:T(512)S(1)} %broadcast_multiply_fusion.2, f32[1152]{0:T(1024)S(1)} %copy-done.37, bf16[1152,3456]{1,0:T(8,128)(2,1)} %weight_ref.3, ...), kind=kOutput, calls=%fused_computation.49 | convolution fusion | flops 4088657408 | bytes 16240128 | tf_op jit(solution)/shard_map/et,de->td/dot_general | solution.py:621
  303.0 13.8 %multiply_reduce_fusion = (f32[1152]{0:T(1024)S(1)}, f32[1152]{0:T(1024)S(1)}, f32[512,1152]{1,0:T(8,128)}, bf16[512,1152]{1,0:T(8,128)(2,1)}) fusion(bf16[512,1152]{1,0:T(8,128)(2,1)S(1)} %copy-done.21, f32[512]{0:T(512)S(1)} %copy-done.54, f32[512,1152]{1,0:T(8,128)} %get-tuple-element.144, f32[512,1152]{1,0:T(8,128)S(1)} %copy-done.12, ...), kind=kOutput, calls=%fused_computation.46 | convolution fusion | flops 5444073472 | bytes 29515776 | tf_op jit(solution)/shard_map/dot_general | solution.py:559
  353.0 25.2 %collective-permute-done.37 = f32[9216]{0:T(1024)S(1)} collective-permute-done((f32[9216]{0:T(1024)S(1)}, f32[9216]{0:T(1024)S(1)}, u32[]{:S(2)}, u32[]{:S(2)}) %collective-permute-start.37) | collective-permute-done | bytes 36896 | tf_op jit(solution)/shard_map/ppermute | solution.py:71
  384.8 9.2 %shard_map.278 = (bf16[2,4,48,864]{3,2,1,0:T(8,128)(2,1)}, bf16[2,4,48,864]{3,2,1,0:T(8,128)(2,1)}, bf16[8,48,864]{2,1,0:T(8,128)(2,1)}, bf16[8,48,864]{2,1,0:T(...) custom-call(bf16[512,1152]{1,0:T(8,128)(2,1)} %get-tuple-element.130.rows_ref.left_ref, ...), custom_call_target="tpu_custom_call" | custom-call | flops 4076863488 | bytes 12238848 | tf_op jit(solution)/shard_map/pallas_call | solution.py:309
  404.2 10.6 %collective-permute-done.47 = bf16[2,144,1152]{2,1,0:T(8,128)(2,1)} collective-permute-done((bf16[2,144,1152]{2,1,0:T(8,128)(2,1)}, bf16[2,144,1152]{2,1,0:T(8,128)(2,1)}, u32[]{:S(2)}, u32[]{:S(2)}) %collective-permute-start.47) | collective-permute-done | bytes 663584 | tf_op jit(solution)/shard_map/ppermute | solution.py:75
  422.3 7.2 %collective-permute-done.24 = bf16[2,2,2,48,864]{4,3,0,2,1:T(8,128)(2,1)S(1)} collective-permute-done((bf16[2,2,2,48,864]{4,3,0,2,1:T(8,128)(2,1)S(1)}, bf16[2,2,2,48,864]{4,3,0,2,1:T(8,128)(2,1)S(1)}, u32[]{:S(2)}, u32[]{:S(2)}) %collective-permute-start.24) | collective-permute-done | bytes 663584 | tf_op jit(solution)/shard_map/ppermute | solution.py:75
  447.2 5.0 %collective-permute-done.31 = bf16[48,864]{1,0:T(8,128)(2,1)S(1)} collective-permute-done((bf16[48,864]{1,0:T(8,128)(2,1)S(1)}, bf16[48,864]{1,0:T(8,128)(2,1)S(1)}, u32[]{:S(2)}, u32[]{:S(2)}) %collective-permute-start.31) | collective-permute-done | bytes 82976 | tf_op jit(solution)/shard_map/ppermute | solution.py:71
  (405 shorter events, 165.7 us)
Async XLA Ops:
  17.1 28.4 %collective-permute-start.2 = (bf16[512,1152]{1,0:T(8,128)(2,1)}, bf16[512,1152]{1,0:T(8,128)(2,1)}, u32[]{:S(2)}, u32[]{:S(2)}) collective-permute-start(bf16[512,1152]{1,0:T(8,128)(2,1)} %param.17), channel_id=1, source_target_pairs={{0,1},{1,0},{2,3},{3,2},{4,5},{5,4},{6,7},{7,6},{8,9},{9,8},{10,11... | collective-permute-start | bytes 3538952 | tf_op jit(solution)/shard_map/ppermute | solution.py:75
  28.2 137.7 %collective-permute-start.4 = (bf16[512,1280]{1,0:T(8,128)(2,1)}, bf16[512,1280]{1,0:T(8,128)(2,1)}, u32[]{:S(2)}, u32[]{:S(2)}) collective-permute-start(bf16[512,1280]{1,0:T(8,128)(2,1)} %fusion.31.right_ref), channel_id=1, source_target_pairs={{0,2},{2,0},{4,6},{6,4},{8,10},{10,8},{12,14},{14,12},{16,18},{18,... | collective-permute-start | bytes 3932168 | tf_op jit(solution)/shard_map/ppermute | solution.py:71
  28.9 201.8 %collective-permute-start.13 = (bf16[8,1152]{1,0:T(8,128)(2,1)}, bf16[8,1152]{1,0:T(8,128)(2,1)}, u32[]{:S(2)}, u32[]{:S(2)}) collective-permute-start(bf16[8,1152]{1,0:T(8,128)(2,1)} %pad_maximum_fusion.10), channel_id=1, source_target_pairs={{0,16},{2,18},{4,20},{6,22},{8,24},{10,26},{12,28},{14,30},{16,0},... | collective-permute-start | bytes 55304 | tf_op jit(solution)/shard_map/ppermute | solution.py:71
  103.6 50.5 %collective-permute-start.5 = (bf16[512,1152]{1,0:T(8,128)(2,1)}, bf16[512,1152]{1,0:T(8,128)(2,1)}, u32[]{:S(2)}, u32[]{:S(2)}) collective-permute-start(bf16[512,1152]{1,0:T(8,128)(2,1)} %add_convert_fusion.4.left_ref), channel_id=1, source_target_pairs={{0,2},{2,0},{4,6},{6,4},{8,10},{10,8},{12,14},{14,12},{16,18},{18,... | collective-permute-start | bytes 3538952 | tf_op jit(solution)/shard_map/ppermute | solution.py:71
  135.6 30.3 %collective-permute-start.3 = (bf16[512,4608]{1,0:T(8,128)(2,1)}, bf16[512,4608]{1,0:T(8,128)(2,1)}, u32[]{:S(2)}, u32[]{:S(2)}) collective-permute-start(bf16[512,4608]{1,0:T(8,128)(2,1)} %get-tuple-element.88.left_ref), channel_id=1, source_target_pairs={{0,2},{2,0},{4,6},{6,4},{8,10},{10,8},{12,14},{14,12},{16,18},{18,... | collective-permute-start | bytes 14155784 | tf_op jit(solution)/shard_map/ppermute | solution.py:71
  154.1 33.1 %collective-permute-start.38 = (bf16[1152,512]{1,0:T(8,128)(2,1)}, bf16[1152,512]{1,0:T(8,128)(2,1)}, u32[]{:S(2)}, u32[]{:S(2)}) collective-permute-start(bf16[1152,512]{1,0:T(8,128)(2,1)} %bitcast.11.left_ref), channel_id=1, source_target_pairs={{0,2},{2,0},{4,6},{6,4},{8,10},{10,8},{12,14},{14,12},{16,18},{18,... | collective-permute-start | bytes 3538952 | tf_op jit(solution)/shard_map/ppermute | solution.py:71
  193.8 33.8 %collective-permute-start.40 = (bf16[2,2,2,144,288]{4,3,0,2,1:T(8,128)(2,1)S(1)}, bf16[2,2,2,144,288]{4,3,0,2,1:T(8,128)(2,1)}, u32[]{:S(2)}, u32[]{:S(2)}) collective-permute-start(bf16[2,2,2,144,288]{4,3,0,2,1:T(8,128)(2,1)S(1)} %copy.67), channel_id=1, source_target_pairs={{0,1},{1,0},{2,3},{3,2},{4,5},{5,4},{6,7},{7,6},{8,9},{9,8},{10,11... | collective-permute-start | bytes 1990664 | tf_op jit(solution)/shard_map/ppermute | solution.py:75
  227.1 53.7 %collective-permute-start.7 = (bf16[2,16,72,512]{3,2,1,0:T(8,128)(2,1)}, bf16[2,16,72,512]{3,2,1,0:T(8,128)(2,1)}, u32[]{:S(2)}, u32[]{:S(2)}) collective-permute-start(bf16[2,16,72,512]{3,2,1,0:T(8,128)(2,1)} %get-tuple-element.49), channel_id=1, source_target_pairs={{0,1},{1,0},{2,3},{3,2},{4,5},{5,4},{6,7},{7,6},{8,9},{9,8},{10,11... | collective-permute-start | bytes 7077896 | tf_op jit(solution)/shard_map/ppermute | solution.py:75
  232.1 152.7 %collective-permute-start.18 = (bf16[512,1152]{1,0:T(8,128)(2,1)}, bf16[512,1152]{1,0:T(8,128)(2,1)}, u32[]{:S(2)}, u32[]{:S(2)}) collective-permute-start(bf16[512,1152]{1,0:T(8,128)(2,1)} %get-tuple-element.130.rows_ref.left_ref), channel_id=1, source_target_pairs={{0,2},{2,0},{4,6},{6,4},{8,10},{10,8},{12,14},{14,12},{16,18},{18,... | collective-permute-start | bytes 3538952 | tf_op jit(solution)/shard_map/ppermute | solution.py:71
  253.7 88.6 %collective-permute-start.50 = (bf16[2,2,2,288,576]{4,3,1,0,2:T(8,128)(2,1)}, bf16[2,2,2,288,576]{4,3,1,0,2:T(8,128)(2,1)}, u32[]{:S(2)}, u32[]{:S(2)}) collective-permute-start(bf16[2,2,2,288,576]{4,3,1,0,2:T(8,128)(2,1)} %copy.72), channel_id=1, source_target_pairs={{0,4},{2,6},{4,0},{6,2},{8,12},{10,14},{12,8},{14,10},{16,20},{18,... | collective-permute-start | bytes 7962632 | tf_op jit(solution)/shard_map/ppermute | solution.py:71
  256.3 89.3 %collective-permute-start.45 = (bf16[2,2,2,144,1152]{4,3,1,0,2:T(8,128)(2,1)}, bf16[2,2,2,144,1152]{4,3,1,0,2:T(8,128)(2,1)}, u32[]{:S(2)}, u32[]{:S(2)}) collective-permute-start(bf16[2,2,2,144,1152]{4,3,1,0,2:T(8,128)(2,1)} %copy.70), channel_id=1, source_target_pairs={{0,8},{2,10},{4,12},{6,14},{8,0},{10,2},{12,4},{14,6},{16,24},{18,... | collective-permute-start | bytes 7962632 | tf_op jit(solution)/shard_map/ppermute | solution.py:71
  286.9 45.0 %collective-permute-start.33 = (f32[9216]{0:T(1024)S(1)}, f32[9216]{0:T(1024)S(1)}, u32[]{:S(2)}, u32[]{:S(2)}) collective-permute-start(f32[9216]{0:T(1024)S(1)} %constant_dynamic-update-slice_fusion.7), channel_id=1, source_target_pairs={{0,1},{1,0},{2,3},{3,2},{4,5},{5,4},{6,7},{7,6},{8,9},{9,8},{10,11... | collective-permute-start | bytes 110600 | tf_op jit(solution)/shard_map/ppermute | solution.py:75
  331.8 53.0 %collective-permute-start.19 = (bf16[1792,512]{1,0:T(8,128)(2,1)S(1)}, bf16[1792,512]{1,0:T(8,128)(2,1)}, u32[]{:S(2)}, u32[]{:S(2)}) collective-permute-start(bf16[1792,512]{1,0:T(8,128)(2,1)S(1)} %fusion.20), channel_id=1, source_target_pairs={{0,2},{2,0},{4,6},{6,4},{8,10},{10,8},{12,14},{14,12},{16,18},{18,... | collective-permute-start | bytes 5505032 | tf_op jit(solution)/shard_map/ppermute | solution.py:71
  345.6 33.7 %collective-permute-start.51 = (bf16[2,2,288,576]{3,2,1,0:T(8,128)(2,1)S(1)}, bf16[2,2,288,576]{3,2,1,0:T(8,128)(2,1)S(1)}, u32[]{:S(2)}, u32[]{:S(2)}) collective-permute-start(bf16[2,2,288,576]{3,2,1,0:T(8,128)(2,1)S(1)} %select_bitcast_fusion), channel_id=1, source_target_pairs={{0,8},{2,10},{4,12},{6,14},{8,0},{10,2},{12,4},{14,6},{16,24},{18,... | collective-permute-start | bytes 3981320 | tf_op jit(solution)/shard_map/ppermute | solution.py:71
  349.9 32.6 %collective-permute-start.46 = (bf16[2,2,144,1152]{3,2,1,0:T(8,128)(2,1)S(1)}, bf16[2,2,144,1152]{3,2,1,0:T(8,128)(2,1)S(1)}, u32[]{:S(2)}, u32[]{:S(2)}) collective-permute-start(bf16[2,2,144,1152]{3,2,1,0:T(8,128)(2,1)S(1)} %select_bitcast_fusion.1), channel_id=1, source_target_pairs={{0,4},{2,6},{4,0},{6,2},{8,12},{10,14},{12,8},{14,10},{16,20},{18,... | collective-permute-start | bytes 3981320 | tf_op jit(solution)/shard_map/ppermute | solution.py:71
  350.6 27.6 %collective-permute-start.37 = (f32[9216]{0:T(1024)S(1)}, f32[9216]{0:T(1024)S(1)}, u32[]{:S(2)}, u32[]{:S(2)}) collective-permute-start(f32[9216]{0:T(1024)S(1)} %add.343), channel_id=1, source_target_pairs={{0,16},{2,18},{4,20},{6,22},{8,24},{10,26},{12,28},{14,30},{16,0},... | collective-permute-start | bytes 110600 | tf_op jit(solution)/shard_map/ppermute | solution.py:71
  381.0 19.6 %collective-permute-start.52 = (bf16[2,288,576]{2,1,0:T(8,128)(2,1)}, bf16[2,288,576]{2,1,0:T(8,128)(2,1)S(1)}, u32[]{:S(2)}, u32[]{:S(2)}) collective-permute-start(bf16[2,288,576]{2,1,0:T(8,128)(2,1)} %slice_bitcast_fusion), channel_id=1, source_target_pairs={{0,1},{1,0},{2,3},{3,2},{4,5},{5,4},{6,7},{7,6},{8,9},{9,8},{10,11... | collective-permute-start | bytes 1990664 | tf_op jit(solution)/shard_map/ppermute | solution.py:75
  384.3 30.5 %collective-permute-start.47 = (bf16[2,144,1152]{2,1,0:T(8,128)(2,1)}, bf16[2,144,1152]{2,1,0:T(8,128)(2,1)}, u32[]{:S(2)}, u32[]{:S(2)}) collective-permute-start(bf16[2,144,1152]{2,1,0:T(8,128)(2,1)} %slice_bitcast_fusion.2), channel_id=1, source_target_pairs={{0,1},{1,0},{2,3},{3,2},{4,5},{5,4},{6,7},{7,6},{8,9},{9,8},{10,11... | collective-permute-start | bytes 1990664 | tf_op jit(solution)/shard_map/ppermute | solution.py:75
  395.4 24.3 %collective-permute-start.28 = (bf16[2,2,2,48,864]{4,3,1,0,2:T(8,128)(2,1)S(1)}, bf16[2,2,2,48,864]{4,3,1,0,2:T(8,128)(2,1)S(1)}, u32[]{:S(2)}, u32[]{:S(2)}) collective-permute-start(bf16[2,2,2,48,864]{4,3,1,0,2:T(8,128)(2,1)S(1)} %copy.65), channel_id=1, source_target_pairs={{0,8},{2,10},{4,12},{6,14},{8,0},{10,2},{12,4},{14,6},{16,24},{18,... | collective-permute-start | bytes 1990664 | tf_op jit(solution)/shard_map/ppermute | solution.py:71
  397.9 22.6 %collective-permute-start.20 = (bf16[2,2,2,48,864]{4,3,1,2,0:T(8,128)(2,1)S(1)}, bf16[2,2,2,48,864]{4,3,1,2,0:T(8,128)(2,1)S(1)}, u32[]{:S(2)}, u32[]{:S(2)}) collective-permute-start(bf16[2,2,2,48,864]{4,3,1,2,0:T(8,128)(2,1)S(1)} %copy.61), channel_id=1, source_target_pairs={{0,4},{2,6},{4,0},{6,2},{8,12},{10,14},{12,8},{14,10},{16,20},{18,... | collective-permute-start | bytes 1990664 | tf_op jit(solution)/shard_map/ppermute | solution.py:71
  398.6 30.9 %collective-permute-start.24 = (bf16[2,2,2,48,864]{4,3,0,2,1:T(8,128)(2,1)S(1)}, bf16[2,2,2,48,864]{4,3,0,2,1:T(8,128)(2,1)S(1)}, u32[]{:S(2)}, u32[]{:S(2)}) collective-permute-start(bf16[2,2,2,48,864]{4,3,0,2,1:T(8,128)(2,1)S(1)} %copy.63), channel_id=1, source_target_pairs={{0,1},{1,0},{2,3},{3,2},{4,5},{5,4},{6,7},{7,6},{8,9},{9,8},{10,11... | collective-permute-start | bytes 1990664 | tf_op jit(solution)/shard_map/ppermute | solution.py:75
  400.8 32.4 %collective-permute-start.53 = (bf16[288,576]{1,0:T(8,128)(2,1)S(1)}, bf16[288,576]{1,0:T(8,128)(2,1)S(1)}, u32[]{:S(2)}, u32[]{:S(2)}) collective-permute-start(bf16[288,576]{1,0:T(8,128)(2,1)S(1)} %select_bitcast_fusion.3), channel_id=1, source_target_pairs={{0,16},{2,18},{4,20},{6,22},{8,24},{10,26},{12,28},{14,30},{16,0},... | collective-permute-start | bytes 995336 | tf_op jit(solution)/shard_map/ppermute | solution.py:71
  416.2 16.7 %collective-permute-start.48 = (bf16[144,1152]{1,0:T(8,128)(2,1)S(1)}, bf16[144,1152]{1,0:T(8,128)(2,1)S(1)}, u32[]{:S(2)}, u32[]{:S(2)}) collective-permute-start(bf16[144,1152]{1,0:T(8,128)(2,1)S(1)} %select_bitcast_fusion.6), channel_id=1, source_target_pairs={{0,16},{2,18},{4,20},{6,22},{8,24},{10,26},{12,28},{14,30},{16,0},... | collective-permute-start | bytes 995336 | tf_op jit(solution)/shard_map/ppermute | solution.py:71
  433.1 21.9 %collective-permute-start.49 = (f32[72,1152]{1,0:T(8,128)S(1)}, f32[72,1152]{1,0:T(8,128)S(1)}, u32[]{:S(2)}, u32[]{:S(2)}) collective-permute-start(f32[72,1152]{1,0:T(8,128)S(1)} %get-tuple-element.103), channel_id=1, source_target_pairs={{0,2},{2,0},{4,6},{6,4},{8,10},{10,8},{12,14},{14,12},{16,18},{18,... | collective-permute-start | bytes 995336 | tf_op jit(solution)/shard_map/ppermute | solution.py:71
  (100 other events, 1016.7 us)
where the time goes:
time: 465 us; the launch traced here: 458 us
  waiting for transfers between devices  118 us (25%)
  Pallas kernels  112 us (24%)
  matrix products  88 us (19%)
  starting transfers between devices  57.3 us (12%)
  other arithmetic  55.2 us (12%)
  local copies, waits for them, and re-layouts  25.2 us (5%)
    ppermute x41, waiting for transfers between devices, swap_bit(): lax.ppermute(value, 'img', [(i, i ^ 1 << bit) for i in range(members)])  60.6 us
    ppermute x13, waiting for transfers between devices, swap_band(): return lax.ppermute(value, 'band', [(0, 1), (1, 0)])  57.6 us
    ppermute x41, starting transfers between devices, swap_bit(): lax.ppermute(value, 'img', [(i, i ^ 1 << bit) for i in range(members)])  39.9 us
    pallas_call x1, Pallas kernels, attend_backward(): pl.pallas_call(functools.partial(attend_back_kernel, score_scale), grid=(...  31.6 us
    pallas_call x3, Pallas kernels, row_product(): pl.pallas_call(functools.partial(product_kernel, left_axis, right_axis, c...  25.8 us
    pallas_call x1, Pallas kernels, attend_forward(): pl.pallas_call(functools.partial(attend_kernel, score_scale), grid=(heads...  21.4 us
    pallas_call x2, Pallas kernels, project_rows(): pl.pallas_call(project_kernel, grid=(width // tile,), in_specs=[pl.BlockS...  21.3 us
    dot_general x1, matrix products, shards(): jnp.einsum('td,fd->tf', grad_mlp, contract_weight, preferred_element_type...  20.6 us
  transfers between devices with their start and end apart: 54, of which 22 were waited for; matrix products, arithmetic and copies ran while one was open for 35% of the time, Pallas kernels for 24%

commit v1 on v0

--- a/solution.py
+++ b/solution.py
@@ -241,6 +241,57 @@
             transcendentals=0,
         ),
     )(rows, weight, bias)
+
+
+def dense_kernel(rows_ref, weight_ref, bias_ref, out_ref):
+    flat = jnp.dot(rows_ref[...], weight_ref[...], preferred_element_type=jnp.float32)
+    out_ref[...] = flat + bias_ref[...].astype(jnp.float32)
+
+
+def dense(rows, weight, bias):
+    depth, width = weight.shape
+    tile = column_tile(width)
+    return pl.pallas_call(
+        dense_kernel,
+        grid=(width // tile,),
+        in_specs=[
+            pl.BlockSpec(rows.shape, lambda n: (0, 0)),
+            pl.BlockSpec((depth, tile), lambda n: (0, n)),
+            pl.BlockSpec((1, tile), lambda n: (0, n)),
+        ],
+        out_specs=pl.BlockSpec((rows.shape[0], tile), lambda n: (0, n)),
+        out_shape=jax.ShapeDtypeStruct((rows.shape[0], width), jnp.float32),
+        cost_estimate=pl.CostEstimate(
+            flops=2 * rows.shape[0] * depth * width,
+            bytes_accessed=2 * depth * width,
+            transcendentals=0,
+        ),
+    )(rows, weight, bias[None, :])
+
+
+def dense_back_kernel(grad_ref, weight_ref, out_ref):
+    flat = jnp.dot(weight_ref[...], grad_ref[...], preferred_element_type=jnp.float32)
+    out_ref[...] = flat.T
+
+
+def dense_back(grad, weight):
+    width, depth = weight.shape
+    tile = column_tile(width)
+    return pl.pallas_call(
+        dense_back_kernel,
+        grid=(width // tile,),
+        in_specs=[
+            pl.BlockSpec(grad.shape, lambda n: (0, 0)),
+            pl.BlockSpec((tile, depth), lambda n: (n, 0)),
+        ],
+        out_specs=pl.BlockSpec((grad.shape[1], tile), lambda n: (0, n)),
+        out_shape=jax.ShapeDtypeStruct((grad.shape[1], width), jnp.float32),
+        cost_estimate=pl.CostEstimate(
+            flops=2 * grad.shape[1] * depth * width,
+            bytes_accessed=2 * depth * width,
+            transcendentals=0,
+        ),
+    )(grad, weight)
 
 
 def product_kernel(
@@ -531,7 +582,9 @@
         flat = project_rows(rows, attend_weight, input_bias, skip)
         return flat.reshape(-1, head_size, slot_count)
 
-    own_heads = project_heads(first_low, 0)
+    own_heads, other_input = lax.optimization_barrier(
+        (project_heads(first_low, 0), other_input)
+    )
     other_shaped = (other_input.astype(jnp.float32) + other_table).reshape(
         image_count, per_image, features
     )
@@ -556,9 +609,7 @@
     ) + expand_bias.astype(jnp.float32)
     activation, gelu_back = jax.vjp(gelu_tanh, expanded)
     activation_low = activation.astype(jnp.bfloat16)
-    mlp_out = jnp.dot(
-        activation_low, contract_weight, preferred_element_type=jnp.float32
-    ) + contract_bias.astype(jnp.float32)
+    mlp_out = dense(activation_low, contract_weight, contract_bias)
     mlp_rows = mlp_out.reshape(image_count, per_image, features)
     result = middle + gate_two[:, None, :] * mlp_rows
     block_output = result.reshape(slot_count, features).astype(jnp.bfloat16)
@@ -592,7 +643,6 @@
     contract_out = scatter_part(*contract_chip, contract_order)
     expand_out = scatter_sum(expand_chip, [expand_order])
     project_chip = chip_product(mixed_low, grad_branch, [project_order], left_axis=1)
-    project_out = scatter_sum(project_chip, [project_order])
     project_bias_grad = jnp.sum(grad_branch.astype(jnp.float32), axis=0)
     grad_mixed = jnp.einsum(
         "td,ed->et", grad_branch, project_weight, preferred_element_type=jnp.float32
@@ -606,6 +656,8 @@
         score_scale,
     )
     grad_pair_far = swap_band(grad_pair_other)
+    grad_pair_far, project_chip = lax.optimization_barrier((grad_pair_far, project_chip))
+    project_out = scatter_sum(project_chip, [project_order])
     grad_pair = grad_pair + grad_pair_far.astype(jnp.float32)
     grad_qkv = jnp.concatenate(
         [
@@ -615,12 +667,11 @@
         axis=0,
     )
     attend_chip = chip_product(first_low, grad_qkv, attend_orders, right_axis=1)
-    attend_out = scatter_sum(attend_chip, attend_orders)
     query_bias_grad = jnp.sum(grad_qkv[:features].astype(jnp.float32), axis=1)
     value_bias_grad = jnp.sum(grad_qkv[2 * features :].astype(jnp.float32), axis=1)
-    grad_first = jnp.einsum(
-        "et,de->td", grad_qkv, attend_weight, preferred_element_type=jnp.float32
-    )
+    grad_first = dense_back(grad_qkv, attend_weight)
+    grad_first, attend_chip = lax.optimization_barrier((grad_first, attend_chip))
+    attend_out = scatter_sum(attend_chip, attend_orders)
     grad_norm_one, grad_shift_one, grad_scale_one = first_back(
         grad_first.reshape(image_count, per_image, features)
     )
@@ -637,9 +688,9 @@
         axis=1,
     )
     grad_halves = grad_modulation.reshape(image_count, 2, -1, features)
+    grad_half_far = swap_band(pick(band, grad_halves[:, 1], grad_halves[:, 0]))
     modulation_grad_half = (
-        pick(band, grad_halves[:, 0], grad_halves[:, 1])
-        + swap_band(pick(band, grad_halves[:, 1], grad_halves[:, 0]))
+        pick(band, grad_halves[:, 0], grad_halves[:, 1]) + grad_half_far
     ).astype(jnp.bfloat16)
     activated_grad_part = jnp.einsum(
         "ikc,dkc->id", modulation_grad_half, modulation_weight, preferred_element_type=jnp.float32

time: 465 us -> 482 us (1.037)
  matrix products: 88 us -> 64.3 us
  Pallas kernels: 112 us -> 134 us
  other arithmetic: 55.2 us -> 68.6 us
  waiting for transfers between devices: 118 us -> 131 us
  local copies, waits for them, and re-layouts: 25.2 us -> 19 us
    ppermute x41, waiting for transfers between devices: 60.6 us -> 85.7 us  [swap_bit(): lax.ppermute(value, 'img', [(i, i ^ 1 << bit) for i in range(members)])]
    dot_general x2 -> x0, matrix products: 25 us -> none  [the longest x1 13.8 us: shards(): jnp.dot(activation_low, contract_weight, preferred_element_type=jnp.float32)]
    pallas_call x0 -> x2, Pallas kernels: none -> 22.1 us  [the longest x1 12.4 us: dense(): pl.pallas_call(dense_kernel, grid=(width // tile,), in_specs=[pl.BlockSpe...]
    ppermute x13, waiting for transfers between devices: 57.6 us -> 45.2 us  [swap_band(): return lax.ppermute(value, 'band', [(0, 1), (1, 0)])]
    reduce_sum x0 -> x2, other arithmetic: none -> 5.46 us  [the longest x1 2.86 us: shards(): grad_gate_two = jnp.sum(upstream * mlp_rows, axis=1)]
    unnamed x154 -> x140, local copies, waits for them, and re-layouts: 10 us -> 4.79 us
  transfers between devices with their start and end apart: 54 -> 54, of which waited for: 22 -> 22; matrix products, arithmetic and copies ran while one was open for 35% -> 28% of each run, Pallas kernels for 24% -> 19%
where the time goes in v1:
time: 482 us; the launch traced here: 476 us
  Pallas kernels  134 us (28%)
  waiting for transfers between devices  131 us (27%)
  other arithmetic  68.6 us (14%)
  matrix products  64.3 us (13%)
  starting transfers between devices  57.6 us (12%)
  local copies, waits for them, and re-layouts  19 us (4%)
    ppermute x41, waiting for transfers between devices, swap_bit(): lax.ppermute(value, 'img', [(i, i ^ 1 << bit) for i in range(members)])  85.7 us
    ppermute x13, waiting for transfers between devices, swap_band(): return lax.ppermute(value, 'band', [(0, 1), (1, 0)])  45.2 us
    ppermute x41, starting transfers between devices, swap_bit(): lax.ppermute(value, 'img', [(i, i ^ 1 << bit) for i in range(members)])  41.4 us
    pallas_call x1, Pallas kernels, attend_backward(): pl.pallas_call(functools.partial(attend_back_kernel, score_scale), grid=(...  31.4 us
    pallas_call x3, Pallas kernels, row_product(): pl.pallas_call(functools.partial(product_kernel, left_axis, right_axis, c...  25.9 us
    pallas_call x1, Pallas kernels, attend_forward(): pl.pallas_call(functools.partial(attend_kernel, score_scale), grid=(heads...  21.4 us
    pallas_call x2, Pallas kernels, project_rows(): pl.pallas_call(project_kernel, grid=(width // tile,), in_specs=[pl.BlockS...  21.3 us
    dot_general x1, matrix products, shards(): jnp.einsum('td,fd->tf', grad_mlp, contract_weight, preferred_element_type...  20.5 us
  transfers between devices with their start and end apart: 54, of which 22 were waited for; matrix products, arithmetic and copies ran while one was open for 28% of the time, Pallas kernels for 19%

profile of v1, /device:TPU:0, one launch (start us, length us, event | category | flops | bytes accessed | tf_op | source)
XLA Modules:
  0.0 476.4 jit_solution(9141255679631010862)
XLA Ops:
  0.7 4.6 fusion.72
  28.9 12.5 %shard_map.272 = bf16[3456,512]{1,0:T(8,128)(2,1)} custom-call(bf16[512,1152]{1,0:T(8,128)(2,1)} %add_convert_fusion.6.rows_ref.left_ref, bf16[1152,3456]{1,0:T(8,128)(2,1)} %weight_ref.7, bf16[1,3456]{1,0:T(2,128)(2,1)} %broadcast_in_dim.29.bias_ref), custom_call_target="tpu_custom_call" | custom-call | flops 4076863488 | bytes 7962624 | tf_op jit(solution)/shard_map/pallas_call | solution.py:228
  51.1 8.8 %shard_map.273 = bf16[2304,512]{1,0:T(8,128)(2,1)} custom-call(bf16[512,1152]{1,0:T(8,128)(2,1)} %add_convert_fusion.5.rows_ref, bf16[1152,3456]{1,0:T(8,128)(2,1)} %weight_ref.7, bf16[1,3456]{1,0:T(2,128)(2,1)} %broadcast_in_dim.29.bias_ref), custom_call_target="tpu_custom_call" | custom-call | flops 2717908992 | bytes 5308416 | tf_op jit(solution)/shard_map/pallas_call | solution.py:228
  59.9 21.4 %shard_map.274 = (bf16[16,72,512]{2,1,0:T(8,128)(2,1)}, f32[16,1,512]{2,1,0:T(1,128)}) custom-call(bf16[48,72,512]{2,1,0:T(8,128)(2,1)} %bitcast.209, bf16[48,72,512]{2,1,0:T(8,128)(2,1)} %bitcast.210, bf16[48,72,512]{2,1,0:T(8,128)(2,1)} %bitcast.211, bf16[32,72,512]{2,1,0:T(8,128)(2,1)} %bitcast.188, bf16[32,72,512]{2,1,0:T(8,128)(2,1)} %bitcast.189, ...), custom_call_target="tpu_custom_call" | custom-call | flops 17179869184 | bytes 7077888 | tf_op jit(solution)/shard_map/pallas_call | solution.py:121
  81.3 5.5 %fusion.90 = (f32[512]{0:T(512)S(1)}, f32[512,1152]{1,0:T(8,128)S(1)}, f32[512,1152]{1,0:T(8,128)}) fusion(f32[512,1152]{1,0:T(8,128)} %copy-done.2, f32[1152]{0:T(1024)S(1)} %get-tuple-element.97, f32[1152]{0:T(1024)S(1)} %convert_element_type.386, bf16[1152,512]{1,0:T(8,128)(2,1)} %bitcast.11.left_ref, bf16[1152,1152]{1,0:T(8,128)(2,1)S(1)} %copy-done), kind=kOutput, calls=%fused_computation.301 | convolution fusion | flops 1361313280 | bytes 10923008 | tf_op jit(solution)/shard_map/et,ed->td/dot_general | solution.py:600
  88.7 11.5 %fusion.93 = f32[512,4608]{1,0:T(8,128)} fusion(bf16[512,1152]{1,0:T(8,128)(2,1)} %add_convert_fusion.4.left_ref, bf16[1152,4608]{1,0:T(8,128)(2,1)} %param.29), kind=kOutput, calls=%fused_computation.304 | convolution fusion | flops 5435817984 | bytes 21233664 | tf_op jit(solution)/shard_map/dot_general | solution.py:607
  100.1 20.5 %convert_reduce_fusion = (f32[4608]{0:T(1024)}, bf16[512,4608]{1,0:T(8,128)(2,1)S(1)}, bf16[512,4608]{1,0:T(8,128)(2,1)}) fusion(f32[512,4608]{1,0:T(8,128)} %fusion.93, f32[4608]{0:T(1024)S(1)} %convert_element_type.388, bf16[512,1152]{1,0:T(8,128)(2,1)} %copy-done.17, bf16[4608,1152]{1,0:T(8,128)(2,1)} %weight_ref.6), kind=kOutput, calls=%fused_computation.10 | convolution fusion | flops 5504232960 | bytes 30707712 | tf_op jit(solution)/shard_map/td,fd->tf/dot_general | solution.py:623
  123.3 11.2 %multiply_reduce_fusion.1 = (f32[1152]{0:T(1024)S(1)}, f32[512]{0:T(512)S(1)}, f32[1152]{0:T(1024)}, f32[512,1152]{1,0:T(8,128)S(1)}) fusion(f32[512,1152]{1,0:T(8,128)S(1)} %get-tuple-element.111, f32[512]{0:T(512)S(1)} %fusion.83, f32[512]{0:T(512)S(1)} %broadcast_multiply_fusion, f32[1152]{0:T(1024)S(1)} %get-tuple-element.96, ...), kind=kOutput, calls=%fused_computation.45 | convolution fusion | flops 5440534016 | bytes 20073984 | tf_op jit(solution)/shard_map/tf,df->td/dot_general | solution.py:629
  139.2 11.2 %shard_map.277 = (bf16[2,4,144,1152]{3,2,1,0:T(8,128)(2,1)}, bf16[2,4,144,1152]{3,2,1,0:T(8,128)(2,1)}) custom-call(bf16[512,1152]{1,0:T(8,128)(2,1)} %add_convert_fusion.4.left_ref, bf16[512,1152]{1,0:T(8,128)(2,1)} %collective-permute-done.5.left_far, bf16[512,2304]{1,0:T(8,128)(2,1)} %pad_maximum_fusion.1.right_ref, ...), custom_call_target="tpu_custom_call" | custom-call | flops 5435817984 | bytes 14745600 | tf_op jit(solution)/shard_map/pallas_call | solution.py:360
  150.4 11.4 %shard_map.276 = (bf16[2,4,288,576]{3,2,1,0:T(8,128)(2,1)}, bf16[2,4,288,576]{3,2,1,0:T(8,128)(2,1)}) custom-call(bf16[512,4608]{1,0:T(8,128)(2,1)} %get-tuple-element.112.rows_ref.left_ref, bf16[512,4608]{1,0:T(8,128)(2,1)} %collective-permute-done.3.left_far, bf16[512,1280]{1,0:T(8,128)(2,1)} %fusion.23.right_ref, ...), custom_call_target="tpu_custom_call" | custom-call | flops 5435817984 | bytes 31850496 | tf_op jit(solution)/shard_map/pallas_call | solution.py:438
  168.4 31.4 %shard_map.278 = (bf16[16,72,512]{2,1,0:T(8,128)(2,1)}, f32[2,16,72,512]{3,2,1,0:T(8,128)}, bf16[2,16,72,512]{3,2,1,0:T(8,128)(2,1)}) custom-call(bf16[48,72,512]{2,1,0:T(8,128)(2,1)} %bitcast.212, bf16[48,72,512]{2,1,0:T(8,128)(2,1)} %bitcast.213, bf16[48,72,512]{2,1,0:T(8,128)(2,1)} %bitcast.214, bf16[32,72,512]{2,1,0:T(8,128)(2,1)} %bitcast.190, ...), custom_call_target="tpu_custom_call" | custom-call | flops 32212254720 | bytes 14155776 | tf_op jit(solution)/shard_map/pallas_call | solution.py:191
  206.7 12.4 %shard_map.275 = f32[512,1152]{1,0:T(8,128)} custom-call(bf16[512,4608]{1,0:T(8,128)(2,1)} %get-tuple-element.112.rows_ref.left_ref, bf16[4608,1152]{1,0:T(8,128)(2,1)} %weight_ref.6, bf16[1,1152]{1,0:T(2,128)(2,1)} %broadcast_in_dim.30.bias_ref), custom_call_target="tpu_custom_call" | custom-call | flops 5435817984 | bytes 10616832 | tf_op jit(solution)/shard_map/pallas_call | solution.py:254
  232.4 5.3 %shard_map.279 = (bf16[8,144,288]{2,1,0:T(8,128)(2,1)}, bf16[8,144,288]{2,1,0:T(8,128)(2,1)}) custom-call(bf16[1152,512]{1,0:T(8,128)(2,1)} %bitcast.11.left_ref, bf16[1152,512]{1,0:T(8,128)(2,1)} %collective-permute-done.8.left_far, bf16[512,768]{1,0:T(8,128)(2,1)} %fusion.27.right_ref, bf16[512,768]{1,0:T(8,128)(2,1)} %collective-permute-done.9.right_far), custom_call_target="tpu_custom_call" | custom-call | flops 1358954496 | bytes 7225344 | tf_op jit(solution)/shard_map/pallas_call | solution.py:360
  237.7 16.1 %collective-permute-done.7 = bf16[2,16,72,512]{3,2,1,0:T(8,128)(2,1)} collective-permute-done((bf16[2,16,72,512]{3,2,1,0:T(8,128)(2,1)}, bf16[2,16,72,512]{3,2,1,0:T(8,128)(2,1)}, u32[]{:S(2)}, u32[]{:S(2)}) %collective-permute-start.7) | collective-permute-done | bytes 2359328 | tf_op jit(solution)/shard_map/ppermute | solution.py:75
  267.3 10.8 %collective-permute-done.35 = f32[9216]{0:T(1024)S(1)} collective-permute-done((f32[9216]{0:T(1024)S(1)}, f32[9216]{0:T(1024)S(1)}, u32[]{:S(2)}, u32[]{:S(2)}) %collective-permute-start.35) | collective-permute-done | bytes 36896 | tf_op jit(solution)/shard_map/ppermute | solution.py:75
  281.4 9.7 %shard_map.280 = f32[512,1152]{1,0:T(8,128)} custom-call(bf16[3456,512]{1,0:T(8,128)(2,1)} %pad_maximum_fusion.grad_ref, bf16[1152,3456]{1,0:T(8,128)(2,1)} %weight_ref.7), custom_call_target="tpu_custom_call" | custom-call | flops 4076863488 | bytes 7962624 | tf_op jit(solution)/shard_map/pallas_call | solution.py:280
  307.8 8.4 %collective-permute-done.41 = bf16[2,2,144,288]{3,2,0,1:T(8,128)(2,1)S(1)} collective-permute-done((bf16[2,2,144,288]{3,2,0,1:T(8,128)(2,1)S(1)}, bf16[2,2,144,288]{3,2,0,1:T(8,128)(2,1)S(1)}, u32[]{:S(2)}, u32[]{:S(2)}) %collective-permute-start.41) | collective-permute-done | bytes 331808 | tf_op jit(solution)/shard_map/ppermute | solution.py:71
  329.0 24.3 %collective-permute-done.43 = bf16[144,288]{1,0:T(8,128)(2,1)S(1)} collective-permute-done((bf16[144,288]{1,0:T(8,128)(2,1)S(1)}, bf16[144,288]{1,0:T(8,128)(2,1)S(1)}, u32[]{:S(2)}, u32[]{:S(2)}) %collective-permute-start.43) | collective-permute-done | bytes 82976 | tf_op jit(solution)/shard_map/ppermute | solution.py:71
  357.8 9.4 %shard_map.281 = (bf16[2,4,48,864]{3,2,1,0:T(8,128)(2,1)}, bf16[2,4,48,864]{3,2,1,0:T(8,128)(2,1)}, bf16[8,48,864]{2,1,0:T(8,128)(2,1)}, bf16[8,48,864]{2,1,0:T(...) custom-call(bf16[512,1152]{1,0:T(8,128)(2,1)} %add_convert_fusion.6.rows_ref.left_ref, ...), custom_call_target="tpu_custom_call" | custom-call | flops 4076863488 | bytes 12238848 | tf_op jit(solution)/shard_map/pallas_call | solution.py:360
  379.9 6.7 %collective-permute-done.46 = bf16[2,2,144,1152]{3,2,1,0:T(8,128)(2,1)} collective-permute-done((bf16[2,2,144,1152]{3,2,1,0:T(8,128)(2,1)}, bf16[2,2,144,1152]{3,2,1,0:T(8,128)(2,1)}, u32[]{:S(2)}, u32[]{:S(2)}) %collective-permute-start.46) | collective-permute-done | bytes 1327136 | tf_op jit(solution)/shard_map/ppermute | solution.py:71
  398.7 11.2 %collective-permute-done.20 = bf16[4,3,1152]{2,0,1:T(4,128)(2,1)S(1)} collective-permute-done((bf16[4,3,1152]{2,0,1:T(4,128)(2,1)S(1)}, bf16[4,3,1152]{2,0,1:T(4,128)(2,1)S(1)}, u32[]{:S(2)}, u32[]{:S(2)}) %collective-permute-start.20) | collective-permute-done | bytes 27680 | tf_op jit(solution)/shard_map/ppermute | solution.py:71
  428.2 7.7 %collective-permute-done.26 = bf16[2,2,2,48,864]{4,3,0,2,1:T(8,128)(2,1)S(1)} collective-permute-done((bf16[2,2,2,48,864]{4,3,0,2,1:T(8,128)(2,1)S(1)}, bf16[2,2,2,48,864]{4,3,0,2,1:T(8,128)(2,1)S(1)}, u32[]{:S(2)}, u32[]{:S(2)}) %collective-permute-start.26) | collective-permute-done | bytes 663584 | tf_op jit(solution)/shard_map/ppermute | solution.py:75
  438.3 12.7 %collective-permute-done.48 = bf16[144,1152]{1,0:T(8,128)(2,1)S(1)} collective-permute-done((bf16[144,1152]{1,0:T(8,128)(2,1)S(1)}, bf16[144,1152]{1,0:T(8,128)(2,1)S(1)}, u32[]{:S(2)}, u32[]{:S(2)}) %collective-permute-start.48) | collective-permute-done | bytes 331808 | tf_op jit(solution)/shard_map/ppermute | solution.py:71
  464.0 5.6 %collective-permute-done.33 = bf16[48,864]{1,0:T(8,128)(2,1)S(1)} collective-permute-done((bf16[48,864]{1,0:T(8,128)(2,1)S(1)}, bf16[48,864]{1,0:T(8,128)(2,1)S(1)}, u32[]{:S(2)}, u32[]{:S(2)}) %collective-permute-start.33) | collective-permute-done | bytes 82976 | tf_op jit(solution)/shard_map/ppermute | solution.py:71
  (395 shorter events, 183.5 us)
Async XLA Ops:
  15.7 28.4 %collective-permute-start.2 = (bf16[512,1152]{1,0:T(8,128)(2,1)}, bf16[512,1152]{1,0:T(8,128)(2,1)}, u32[]{:S(2)}, u32[]{:S(2)}) collective-permute-start(bf16[512,1152]{1,0:T(8,128)(2,1)} %param.17), channel_id=1, source_target_pairs={{0,1},{1,0},{2,3},{3,2},{4,5},{5,4},{6,7},{7,6},{8,9},{9,8},{10,11... | collective-permute-start | bytes 3538952 | tf_op jit(solution)/shard_map/ppermute | solution.py:75
  20.2 21.2 %collective-permute-start.16 = (bf16[4,1152]{1,0:T(4,128)(2,1)S(1)}, bf16[4,1152]{1,0:T(4,128)(2,1)S(1)}, u32[]{:S(2)}, u32[]{:S(2)}) collective-permute-start(bf16[4,1152]{1,0:T(4,128)(2,1)S(1)} %pad_maximum_fusion.12), channel_id=1, source_target_pairs={{0,8},{2,10},{4,12},{6,14},{8,0},{10,2},{12,4},{14,6},{16,24},{18,... | collective-permute-start | bytes 27656 | tf_op jit(solution)/shard_map/ppermute | solution.py:71
  26.8 123.6 %collective-permute-start.4 = (bf16[512,1280]{1,0:T(8,128)(2,1)}, bf16[512,1280]{1,0:T(8,128)(2,1)}, u32[]{:S(2)}, u32[]{:S(2)}) collective-permute-start(bf16[512,1280]{1,0:T(8,128)(2,1)} %fusion.23.right_ref), channel_id=1, source_target_pairs={{0,2},{2,0},{4,6},{6,4},{8,10},{10,8},{12,14},{14,12},{16,18},{18,... | collective-permute-start | bytes 3932168 | tf_op jit(solution)/shard_map/ppermute | solution.py:71
  88.7 50.5 %collective-permute-start.5 = (bf16[512,1152]{1,0:T(8,128)(2,1)}, bf16[512,1152]{1,0:T(8,128)(2,1)}, u32[]{:S(2)}, u32[]{:S(2)}) collective-permute-start(bf16[512,1152]{1,0:T(8,128)(2,1)} %add_convert_fusion.4.left_ref), channel_id=1, source_target_pairs={{0,2},{2,0},{4,6},{6,4},{8,10},{10,8},{12,14},{14,12},{16,18},{18,... | collective-permute-start | bytes 3538952 | tf_op jit(solution)/shard_map/ppermute | solution.py:71
  120.7 29.7 %collective-permute-start.3 = (bf16[512,4608]{1,0:T(8,128)(2,1)}, bf16[512,4608]{1,0:T(8,128)(2,1)}, u32[]{:S(2)}, u32[]{:S(2)}) collective-permute-start(bf16[512,4608]{1,0:T(8,128)(2,1)} %get-tuple-element.112.rows_ref.left_ref), channel_id=1, source_target_pairs={{0,2},{2,0},{4,6},{6,4},{8,10},{10,8},{12,14},{14,12},{16,18},{18,... | collective-permute-start | bytes 14155784 | tf_op jit(solution)/shard_map/ppermute | solution.py:71
  199.8 54.0 %collective-permute-start.7 = (bf16[2,16,72,512]{3,2,1,0:T(8,128)(2,1)}, bf16[2,16,72,512]{3,2,1,0:T(8,128)(2,1)}, u32[]{:S(2)}, u32[]{:S(2)}) collective-permute-start(bf16[2,16,72,512]{3,2,1,0:T(8,128)(2,1)} %get-tuple-element.63), channel_id=1, source_target_pairs={{0,1},{1,0},{2,3},{3,2},{4,5},{5,4},{6,7},{7,6},{8,9},{9,8},{10,11... | collective-permute-start | bytes 7077896 | tf_op jit(solution)/shard_map/ppermute | solution.py:75
  204.6 153.2 %collective-permute-start.10 = (bf16[512,1152]{1,0:T(8,128)(2,1)}, bf16[512,1152]{1,0:T(8,128)(2,1)}, u32[]{:S(2)}, u32[]{:S(2)}) collective-permute-start(bf16[512,1152]{1,0:T(8,128)(2,1)} %add_convert_fusion.6.rows_ref.left_ref), channel_id=1, source_target_pairs={{0,2},{2,0},{4,6},{6,4},{8,10},{10,8},{12,14},{14,12},{16,18},{18,... | collective-permute-start | bytes 3538952 | tf_op jit(solution)/shard_map/ppermute | solution.py:71
  206.7 24.0 %collective-permute-start.8 = (bf16[1152,512]{1,0:T(8,128)(2,1)}, bf16[1152,512]{1,0:T(8,128)(2,1)}, u32[]{:S(2)}, u32[]{:S(2)}) collective-permute-start(bf16[1152,512]{1,0:T(8,128)(2,1)} %bitcast.11.left_ref), channel_id=1, source_target_pairs={{0,2},{2,0},{4,6},{6,4},{8,10},{10,8},{12,14},{14,12},{16,18},{18,... | collective-permute-start | bytes 3538952 | tf_op jit(solution)/shard_map/ppermute | solution.py:71
  223.0 82.2 %collective-permute-start.50 = (bf16[2,2,2,288,576]{4,3,1,0,2:T(8,128)(2,1)}, bf16[2,2,2,288,576]{4,3,1,0,2:T(8,128)(2,1)}, u32[]{:S(2)}, u32[]{:S(2)}) collective-permute-start(bf16[2,2,2,288,576]{4,3,1,0,2:T(8,128)(2,1)} %copy.72), channel_id=1, source_target_pairs={{0,4},{2,6},{4,0},{6,2},{8,12},{10,14},{12,8},{14,10},{16,20},{18,... | collective-permute-start | bytes 7962632 | tf_op jit(solution)/shard_map/ppermute | solution.py:71
  230.8 95.7 %collective-permute-start.45 = (bf16[2,2,2,144,1152]{4,3,1,0,2:T(8,128)(2,1)}, bf16[2,2,2,144,1152]{4,3,1,0,2:T(8,128)(2,1)}, u32[]{:S(2)}, u32[]{:S(2)}) collective-permute-start(bf16[2,2,2,144,1152]{4,3,1,0,2:T(8,128)(2,1)} %copy.70), channel_id=1, source_target_pairs={{0,8},{2,10},{4,12},{6,14},{8,0},{10,2},{12,4},{14,6},{16,24},{18,... | collective-permute-start | bytes 7962632 | tf_op jit(solution)/shard_map/ppermute | solution.py:71
  256.0 46.1 %collective-permute-start.40 = (bf16[2,2,2,144,288]{4,3,0,2,1:T(8,128)(2,1)}, bf16[2,2,2,144,288]{4,3,0,2,1:T(8,128)(2,1)}, u32[]{:S(2)}, u32[]{:S(2)}) collective-permute-start(bf16[2,2,2,144,288]{4,3,0,2,1:T(8,128)(2,1)} %copy.68), channel_id=1, source_target_pairs={{0,1},{1,0},{2,3},{3,2},{4,5},{5,4},{6,7},{7,6},{8,9},{9,8},{10,11... | collective-permute-start | bytes 1990664 | tf_op jit(solution)/shard_map/ppermute | solution.py:75
  300.9 56.9 %collective-permute-start.11 = (bf16[1792,512]{1,0:T(8,128)(2,1)S(1)}, bf16[1792,512]{1,0:T(8,128)(2,1)}, u32[]{:S(2)}, u32[]{:S(2)}) collective-permute-start(bf16[1792,512]{1,0:T(8,128)(2,1)S(1)} %fusion.16), channel_id=1, source_target_pairs={{0,2},{2,0},{4,6},{6,4},{8,10},{10,8},{12,14},{14,12},{16,18},{18,... | collective-permute-start | bytes 5505032 | tf_op jit(solution)/shard_map/ppermute | solution.py:71
  318.2 37.9 %collective-permute-start.51 = (bf16[2,2,288,576]{3,2,1,0:T(8,128)(2,1)S(1)}, bf16[2,2,288,576]{3,2,1,0:T(8,128)(2,1)S(1)}, u32[]{:S(2)}, u32[]{:S(2)}) collective-permute-start(bf16[2,2,288,576]{3,2,1,0:T(8,128)(2,1)S(1)} %select_bitcast_fusion), channel_id=1, source_target_pairs={{0,8},{2,10},{4,12},{6,14},{8,0},{10,2},{12,4},{14,6},{16,24},{18,... | collective-permute-start | bytes 3981320 | tf_op jit(solution)/shard_map/ppermute | solution.py:71
  323.6 29.7 %collective-permute-start.43 = (bf16[144,288]{1,0:T(8,128)(2,1)S(1)}, bf16[144,288]{1,0:T(8,128)(2,1)S(1)}, u32[]{:S(2)}, u32[]{:S(2)}) collective-permute-start(bf16[144,288]{1,0:T(8,128)(2,1)S(1)} %select_bitcast_fusion.10), channel_id=1, source_target_pairs={{0,16},{2,18},{4,20},{6,22},{8,24},{10,26},{12,28},{14,30},{16,0},... | collective-permute-start | bytes 248840 | tf_op jit(solution)/shard_map/ppermute | solution.py:71
  354.7 31.8 %collective-permute-start.46 = (bf16[2,2,144,1152]{3,2,1,0:T(8,128)(2,1)}, bf16[2,2,144,1152]{3,2,1,0:T(8,128)(2,1)}, u32[]{:S(2)}, u32[]{:S(2)}) collective-permute-start(bf16[2,2,144,1152]{3,2,1,0:T(8,128)(2,1)} %select_bitcast_fusion.1), channel_id=1, source_target_pairs={{0,4},{2,6},{4,0},{6,2},{8,12},{10,14},{12,8},{14,10},{16,20},{18,... | collective-permute-start | bytes 3981320 | tf_op jit(solution)/shard_map/ppermute | solution.py:71
  377.6 43.5 %collective-permute-start.52 = (bf16[2,288,576]{2,1,0:T(8,128)(2,1)S(1)}, bf16[2,288,576]{2,1,0:T(8,128)(2,1)S(1)}, u32[]{:S(2)}, u32[]{:S(2)}) collective-permute-start(bf16[2,288,576]{2,1,0:T(8,128)(2,1)S(1)} %slice_bitcast_fusion), channel_id=1, source_target_pairs={{0,1},{1,0},{2,3},{3,2},{4,5},{5,4},{6,7},{7,6},{8,9},{9,8},{10,11... | collective-permute-start | bytes 1990664 | tf_op jit(solution)/shard_map/ppermute | solution.py:75
  389.2 33.6 %collective-permute-start.47 = (bf16[2,144,1152]{2,1,0:T(8,128)(2,1)S(1)}, bf16[2,144,1152]{2,1,0:T(8,128)(2,1)S(1)}, u32[]{:S(2)}, u32[]{:S(2)}) collective-permute-start(bf16[2,144,1152]{2,1,0:T(8,128)(2,1)S(1)} %slice_bitcast_fusion.2), channel_id=1, source_target_pairs={{0,1},{1,0},{2,3},{3,2},{4,5},{5,4},{6,7},{7,6},{8,9},{9,8},{10,11... | collective-permute-start | bytes 1990664 | tf_op jit(solution)/shard_map/ppermute | solution.py:75
  390.8 33.8 %collective-permute-start.30 = (bf16[2,2,2,48,864]{4,3,1,0,2:T(8,128)(2,1)S(1)}, bf16[2,2,2,48,864]{4,3,1,0,2:T(8,128)(2,1)S(1)}, u32[]{:S(2)}, u32[]{:S(2)}) collective-permute-start(bf16[2,2,2,48,864]{4,3,1,0,2:T(8,128)(2,1)S(1)} %copy.66), channel_id=1, source_target_pairs={{0,8},{2,10},{4,12},{6,14},{8,0},{10,2},{12,4},{14,6},{16,24},{18,... | collective-permute-start | bytes 1990664 | tf_op jit(solution)/shard_map/ppermute | solution.py:71
  394.7 31.8 %collective-permute-start.22 = (bf16[2,2,2,48,864]{4,3,1,2,0:T(8,128)(2,1)S(1)}, bf16[2,2,2,48,864]{4,3,1,2,0:T(8,128)(2,1)S(1)}, u32[]{:S(2)}, u32[]{:S(2)}) collective-permute-start(bf16[2,2,2,48,864]{4,3,1,2,0:T(8,128)(2,1)S(1)} %copy.62), channel_id=1, source_target_pairs={{0,4},{2,6},{4,0},{6,2},{8,12},{10,14},{12,8},{14,10},{16,20},{18,... | collective-permute-start | bytes 1990664 | tf_op jit(solution)/shard_map/ppermute | solution.py:71
  421.3 30.0 %collective-permute-start.53 = (bf16[288,576]{1,0:T(8,128)(2,1)S(1)}, bf16[288,576]{1,0:T(8,128)(2,1)S(1)}, u32[]{:S(2)}, u32[]{:S(2)}) collective-permute-start(bf16[288,576]{1,0:T(8,128)(2,1)S(1)} %select_bitcast_fusion.3), channel_id=1, source_target_pairs={{0,16},{2,18},{4,20},{6,22},{8,24},{10,26},{12,28},{14,30},{16,0},... | collective-permute-start | bytes 995336 | tf_op jit(solution)/shard_map/ppermute | solution.py:71
  423.1 28.0 %collective-permute-start.48 = (bf16[144,1152]{1,0:T(8,128)(2,1)S(1)}, bf16[144,1152]{1,0:T(8,128)(2,1)S(1)}, u32[]{:S(2)}, u32[]{:S(2)}) collective-permute-start(bf16[144,1152]{1,0:T(8,128)(2,1)S(1)} %select_bitcast_fusion.6), channel_id=1, source_target_pairs={{0,16},{2,18},{4,20},{6,22},{8,24},{10,26},{12,28},{14,30},{16,0},... | collective-permute-start | bytes 995336 | tf_op jit(solution)/shard_map/ppermute | solution.py:71
  424.9 27.5 %collective-permute-start.31 = (bf16[2,2,48,864]{3,2,1,0:T(8,128)(2,1)S(1)}, bf16[2,2,48,864]{3,2,1,0:T(8,128)(2,1)S(1)}, u32[]{:S(2)}, u32[]{:S(2)}) collective-permute-start(bf16[2,2,48,864]{3,2,1,0:T(8,128)(2,1)S(1)} %select_bitcast_fusion.4), channel_id=1, source_target_pairs={{0,4},{2,6},{4,0},{6,2},{8,12},{10,14},{12,8},{14,10},{16,20},{18,... | collective-permute-start | bytes 995336 | tf_op jit(solution)/shard_map/ppermute | solution.py:71
  426.6 27.5 %collective-permute-start.23 = (bf16[2,2,48,864]{3,2,0,1:T(8,128)(2,1)S(1)}, bf16[2,2,48,864]{3,2,0,1:T(8,128)(2,1)S(1)}, u32[]{:S(2)}, u32[]{:S(2)}) collective-permute-start(bf16[2,2,48,864]{3,2,0,1:T(8,128)(2,1)S(1)} %slice_bitcast_fusion.4), channel_id=1, source_target_pairs={{0,1},{1,0},{2,3},{3,2},{4,5},{5,4},{6,7},{7,6},{8,9},{9,8},{10,11... | collective-permute-start | bytes 995336 | tf_op jit(solution)/shard_map/ppermute | solution.py:75
  451.3 22.1 %collective-permute-start.49 = (f32[72,1152]{1,0:T(8,128)S(1)}, f32[72,1152]{1,0:T(8,128)S(1)}, u32[]{:S(2)}, u32[]{:S(2)}) collective-permute-start(f32[72,1152]{1,0:T(8,128)S(1)} %get-tuple-element.127), channel_id=1, source_target_pairs={{0,2},{2,0},{4,6},{6,4},{8,10},{10,8},{12,14},{14,12},{16,18},{18,... | collective-permute-start | bytes 995336 | tf_op jit(solution)/shard_map/ppermute | solution.py:71
  (93 other events, 939.7 us)
